TPU v7x, 8 devices: a whole 2x2x1 slice. The times are simulated.
8 devices in a mesh: dp: 1 (over z), tp: 2 (over y), sq: 4 (over x, core).
Axes of the slice: x: 2, y: 2, z: 1, core: 2. Of those that a mesh axis runs over, the one named last changes fastest.
Arguments:
- hidden: bfloat16 [256, 2048], P('dp')
- cache_lens: int32 [256], P('dp')
- k_cache: bfloat16 [256, 1024, 128], P('dp', 'sq')
- v_cache: bfloat16 [256, 1024, 128], P('dp', 'sq')
- ln_gain: float32 [2048], replicated
- ln_bias: float32 [2048], replicated
- w_query: bfloat16 [2048, 2048], P(None, 'tp')
- b_query: float32 [2048], P('tp')
- w_kv: bfloat16 [2048, 256], replicated
- b_kv: float32 [256], replicated
- w_out: bfloat16 [2048, 2048], P('tp')
- b_out: float32 [2048], replicated
Outputs:
- output 1: bfloat16 [256, 2048], P('dp')
- output 2: bfloat16 [256, 1024, 128], P('dp', 'sq')
- output 3: bfloat16 [256, 1024, 128], P('dp', 'sq')
All inputs are finite; a program needn't handle non-finite values.
Results may differ from a plain program's by a relative error of at most 0.00351369.
Values sent between devices are 32-bit elements.
A program may use at most 1 GiB of HBM per device.

v0:
```python
import jax
import jax.numpy as jnp
from jax import lax
from jax.sharding import PartitionSpec as P


def layer_norm(x_rows, ln_gain, ln_bias):
    x_wide = x_rows.astype(jnp.float32)
    mean_val = jnp.mean(x_wide, axis=-1, keepdims=True)
    centered = x_wide - mean_val
    variance = jnp.mean(centered * centered, axis=-1, keepdims=True)
    normed = centered * lax.rsqrt(variance + 1e-5)
    return (normed * ln_gain + ln_bias).astype(jnp.bfloat16)


def solution(mesh):
    def local_step(hidden, cache_lens, k_cache, v_cache, ln_gain, ln_bias, w_query, b_query, w_kv, b_kv, w_out, b_out):
        batch, pos_local, head_dim = k_cache.shape
        heads_local = w_query.shape[1] // head_dim
        normed = layer_norm(hidden, ln_gain, ln_bias)
        query = (jnp.dot(normed, w_query, preferred_element_type=jnp.float32) + b_query).astype(jnp.bfloat16)
        query = query.reshape(batch, heads_local, head_dim)
        key_val = (jnp.dot(normed, w_kv, preferred_element_type=jnp.float32) + b_kv).astype(jnp.bfloat16)
        first_pos = lax.axis_index("sq") * pos_local
        positions = first_pos + lax.broadcasted_iota(jnp.int32, (1, pos_local), 1)
        at_slot = (positions == cache_lens[:, None])[:, :, None]
        key_new = jnp.where(at_slot, key_val[:, None, :head_dim], k_cache)
        val_new = jnp.where(at_slot, key_val[:, None, head_dim:], v_cache)
        scores = jnp.einsum("bnd,btd->bnt", query, key_new, preferred_element_type=jnp.float32) * (head_dim ** -0.5)
        valid = (positions <= cache_lens[:, None])[:, None, :]
        scores = jnp.where(valid, scores, -1e30)
        local_max = jnp.max(scores, axis=-1, keepdims=True)
        global_max = lax.pmax(local_max, "sq")
        weights = jnp.where(valid, jnp.exp(scores - global_max), 0.0)
        denominator = lax.psum(jnp.sum(weights, axis=-1, keepdims=True), "sq")
        numerator = lax.psum(jnp.einsum("bnt,btd->bnd", weights.astype(jnp.bfloat16), val_new, preferred_element_type=jnp.float32), "sq")
        attended = (numerator / denominator).astype(jnp.bfloat16).reshape(batch, heads_local * head_dim)
        part_sum = jnp.dot(attended, w_out, preferred_element_type=jnp.float32)
        projected = lax.psum(part_sum, "tp")
        out_hidden = (hidden.astype(jnp.float32) + projected + b_out).astype(jnp.bfloat16)
        return out_hidden, key_new, val_new

    cache_spec = P("dp", "sq", None)
    row_spec = P("dp", None)
    in_specs = (row_spec, P("dp"), cache_spec, cache_spec, P(None), P(None), P(None, "tp"), P("tp"), P(None, None), P(None), P("tp", None), P(None))
    out_specs = (row_spec, cache_spec, cache_spec)
    return jax.shard_map(local_step, mesh=mesh, in_specs=in_specs, out_specs=out_specs, check_vma=False)
```

profile of v0, /device:TPU:0, one launch (start us, length us, event | category | flops | bytes accessed | tf_op | source)
XLA Modules:
  0.0 173.5 jit_solution(8622052499564978420)
XLA Ops:
  7.2 0.0 copy-start
  7.2 0.0 copy-start.6
  7.2 0.0 copy-start.7
  7.2 0.0 copy-start.8
  7.2 0.0 all-reduce.3.cloned.1.call-start
  7.3 0.0 copy-start.2
  7.3 1.6 convert_reduce_fusion
  8.9 2.4 %fusion.2 = f32[256]{0:T(256)S(1)} fusion(bf16[256,2048]{1,0:T(8,128)(2,1)} %param.12, f32[256]{0:T(256)S(1)} %broadcast_multiply_fusion), kind=kLoop, calls=%fused_computation.7 | loop fusion | flops 2096896 | bytes 1050624 | tf_op jit(solution)/shard_map/reduce_sum | solution.py:11
  11.3 0.0 copy-done
  11.3 0.0 copy-done.6
  11.3 0.0 copy-done.7
  11.3 0.0 copy-done.8
  11.3 2.4 %fusion.13 = bf16[256,256]{1,0:T(8,128)(2,1)S(1)} fusion(bf16[2048,256]{1,0:T(8,128)(2,1)S(1)} %copy-done, f32[256]{0:T(256)S(1)} %copy-done.8, bf16[256,2048]{1,0:T(8,128)(2,1)} %param.12, f32[2048]{0:T(1024)S(1)} %copy-done.6, f32[2048]{0:T(1024)S(1)} %copy-done.7, f32[256]{0:T(256)S(1)} %add_rsqrt_fusion, f32[256]{0:T(256)S(1)} %broadcast_multiply_fusion), kind=kOutput, calls=%fused_computation.22 | convolution fusion | flops 271712256 | bytes 2247680 | tf_op jit(solution)/shard_map/dot_general | solution.py:23
  13.7 0.0 copy-start.5
  13.7 3.8 %fusion.12 = bf16[32,8,8,128]{3,1,2,0:T(8,128)(2,1)S(1)} fusion(bf16[2048,1024]{1,0:T(8,128)(2,1)} %param.18, f32[1024]{0:T(1024)} %param.19, bf16[256,2048]{1,0:T(8,128)(2,1)} %param.12, f32[2048]{0:T(1024)S(1)} %copy-done.6, f32[2048]{0:T(1024)S(1)} %copy-done.7, f32[256]{0:T(256)S(1)} %add_rsqrt_fusion, f32[256]{0:T(256)S(1)} %broadcast_multiply_fusion), kind=kOutput, calls=%fused_computation.20 | convolution fusion | flops 1077411840 | bytes 5789696 | tf_op jit(solution)/shard_map/dot_general | solution.py:21
  17.6 0.1 copy.15
  17.7 0.0 copy-done.5
  17.7 0.1 broadcast_compare_fusion.1
  17.8 0.0 copy-done.2
  17.8 17.4 %broadcast_select_fusion.1 = (bf16[256,256,128]{2,1,0:T(8,128)(2,1)}, bf16[256,256,128]{2,1,0:T(8,128)(2,1)}) fusion(bf16[256,256,128]{2,1,0:T(8,128)(2,1)S(1)} %copy-done.2, pred[256,256]{1,0:T(8,128)(4,1)S(1)} %get-tuple-element.8, bf16[256,128]{1,0:T(8,128)(2,1)S(1)} %get-tuple-element.3, bf16[256,256,128]{2,1,0:T(8,128)(2,1)} %param.15, ...), kind=kLoop, calls=%fused_computation.1 | loop fusion | flops 16777216 | bytes 67305472 | tf_op jit(solution)/shard_map/jit(_where)/select_n | solution.py:27
  35.2 8.1 %fusion.8 = (f32[256,8]{1,0:T(8,128)S(1)}, f32[256,8,256]{2,1,0:T(8,128)S(1)}) fusion(pred[256,256]{1,0:T(8,128)(4,1)S(1)} %get-tuple-element.7, bf16[256,8,128]{2,1,0:T(8,128)(2,1)S(1)} %bitcast.13, bf16[256,256,128]{2,1,0:T(8,128)(2,1)} %get-tuple-element.5), kind=kOutput, calls=%fused_computation.15 | convolution fusion | flops 135788544 | bytes 19472384 | tf_op jit(solution)/shard_map/bnd,btd->bnt/dot_general | solution.py:29
  43.4 14.8 %pmax.7 = f32[256,8]{1,0:T(8,128)S(1)} all-reduce(f32[256,8]{1,0:T(8,128)S(1)} %get-tuple-element.9), channel_id=1, replica_groups=mesh['dp'=1,'tp'=2,'sq'=4] {'sq'}, use_global_device_ids=true, to_apply=%region_3.4 | all-reduce | flops 2048 | bytes 16384 | tf_op jit(solution)/shard_map/pmax | solution.py:33
  58.2 9.1 %fusion.14 = f32[256,8,128]{2,1,0:T(8,128)} fusion(bf16[256,256,128]{2,1,0:T(8,128)(2,1)} %get-tuple-element.6, f32[256,8,256]{2,1,0:T(8,128)S(1)} %get-tuple-element.10, f32[256,8]{1,0:T(8,128)S(1)} %pmax.7, pred[256,256]{1,0:T(8,128)(4,1)S(1)} %get-tuple-element.7), kind=kOutput, calls=%fused_computation.23 | convolution fusion | flops 136839168 | bytes 19996672 | tf_op jit(solution)/shard_map/bnt,btd->bnd/dot_general | solution.py:36
  67.4 0.0 all-reduce.3.cloned.1.call-update
  67.4 0.0 all-reduce.5.cloned.1.call-start
  67.4 1.3 fusion.9
  68.7 14.6 %psum.22 = f32[256,8]{1,0:T(8,128)S(1)} all-reduce(f32[256,8]{1,0:T(8,128)S(1)} %fusion.9), channel_id=1, replica_groups=mesh['dp'=1,'tp'=2,'sq'=4] {'sq'}, use_global_device_ids=true, to_apply=%region_6.7 | all-reduce | flops 2048 | bytes 16384 | tf_op jit(solution)/shard_map/psum | solution.py:35
  83.4 16.6 %all-reduce.3.cloned.1.call-done = f32[256,8,128]{2,1,0:T(8,128)} async-done(((f32[256,8,128]{2,1,0:T(8,128)}), f32[256,8,128]{2,1,0:T(8,128)}) %all-reduce.3.cloned.1.call-update) | async-done | bytes 1048592 | tf_op jit(solution)/shard_map/psum | solution.py:36
  99.9 1.6 divide_convert_fusion
  101.5 4.7 %fusion.21 = f32[256,2048]{1,0:T(8,128)} fusion(bf16[1024,2048]{1,0:T(8,128)(2,1)} %param.22, bf16[32,8,8,128]{3,2,1,0:T(8,128)(2,1)S(1)} %bitcast.14), kind=kOutput, calls=%fused_computation.30 | convolution fusion | flops 1073741824 | bytes 6815744 | tf_op jit(solution)/shard_map/dot_general | solution.py:38
  106.3 0.0 copy-start.3
  106.3 0.0 copy-start.4
  106.3 0.0 all-reduce.5.cloned.1.call-update
  106.3 0.0 copy-start.1
  106.3 57.5 %all-reduce.5.cloned.1.call-done = f32[256,2048]{1,0:T(8,128)} async-done(((f32[256,2048]{1,0:T(8,128)}), f32[256,2048]{1,0:T(8,128)}) %all-reduce.5.cloned.1.call-update) | async-done | bytes 2097168 | tf_op jit(solution)/shard_map/psum | solution.py:39
  163.8 0.0 copy-done.3
  163.8 0.0 copy-done.4
  163.8 2.9 %fusion.7 = bf16[256,2048]{1,0:T(8,128)(2,1)} fusion(f32[256,2048]{1,0:T(8,128)} %all-reduce.5.cloned.1.call-done, bf16[256,2048]{1,0:T(8,128)(2,1)S(1)} %copy-done.3, f32[2048]{0:T(1024)S(1)} %copy-done.4), kind=kLoop, calls=%fused_computation.12 | loop fusion | flops 2097152 | bytes 4202496 | tf_op jit(solution)/shard_map/convert_element_type | solution.py:40
  166.7 0.0 copy-done.1
  (4 shorter events, 0.0 us)
Async XLA Ops:
  7.2 4.1 %copy-start = (bf16[2048,256]{1,0:T(8,128)(2,1)S(1)}, bf16[2048,256]{1,0:T(8,128)(2,1)}, u32[]{:S(2)}) copy-start(bf16[2048,256]{1,0:T(8,128)(2,1)} %param.20) | copy-start | bytes 3145732
  7.2 4.1 %copy-start.6 = (f32[2048]{0:T(1024)S(1)}, f32[2048]{0:T(1024)}, u32[]{:S(2)}) copy-start(f32[2048]{0:T(1024)} %param.17) | copy-start | bytes 24580
  7.2 4.1 %copy-start.7 = (f32[2048]{0:T(1024)S(1)}, f32[2048]{0:T(1024)}, u32[]{:S(2)}) copy-start(f32[2048]{0:T(1024)} %param.16) | copy-start | bytes 24580
  7.2 4.1 %copy-start.8 = (f32[256]{0:T(256)S(1)}, f32[256]{0:T(256)}, u32[]{:S(2)}) copy-start(f32[256]{0:T(256)} %param.21) | copy-start | bytes 3076
  7.2 92.7 %all-reduce.3.cloned.1.call-start = ((), (), s32[]{:S(2)}) async-start(), calls=%async_computation | async-start | bytes 2097152 | tf_op jit(solution)/shard_map/psum | solution.py:36
  7.3 10.5 %copy-start.2 = (bf16[256,256,128]{2,1,0:T(8,128)(2,1)S(1)}, bf16[256,256,128]{2,1,0:T(8,128)(2,1)}, u32[]{:S(2)}) copy-start(bf16[256,256,128]{2,1,0:T(8,128)(2,1)} %param.14) | copy-start | bytes 50331652
  13.7 3.9 %copy-start.5 = (s32[256]{0:T(256)S(1)}, s32[256]{0:T(256)}, u32[]{:S(2)}) copy-start(s32[256]{0:T(256)} %param.13) | copy-start | bytes 3076
  67.4 96.4 %all-reduce.5.cloned.1.call-start = ((), (), s32[]{:S(2)}) async-start(), calls=%async_computation.1 | async-start | bytes 4194304 | tf_op jit(solution)/shard_map/psum | solution.py:39
  106.3 57.6 %copy-start.3 = (bf16[256,2048]{1,0:T(8,128)(2,1)S(1)}, bf16[256,2048]{1,0:T(8,128)(2,1)}, u32[]{:S(2)}) copy-start(bf16[256,2048]{1,0:T(8,128)(2,1)} %param.12) | copy-start | bytes 3145732
  106.3 57.6 %copy-start.4 = (f32[2048]{0:T(1024)S(1)}, f32[2048]{0:T(1024)}, u32[]{:S(2)}) copy-start(f32[2048]{0:T(1024)} %param.23) | copy-start | bytes 24580
  106.3 60.4 %copy-start.1 = (bf16[2048,256]{1,0:T(8,128)(2,1)S(1)}, bf16[2048,256]{1,0:T(8,128)(2,1)}, u32[]{:S(2)}) copy-start(bf16[2048,256]{1,0:T(8,128)(2,1)} %param.20) | copy-start | bytes 3145732
Sparse Core Ops, SparseCore 0:
  67.5 32.3 all-reduce.2
  106.4 57.3 all-reduce.4
where the time goes:
time: 174 us
  waiting for transfers between devices  74.1 us (43%)
  blocking collectives  29.5 us (17%)
  matrix products  28.2 us (16%)
  other arithmetic  27.3 us (16%)
  between operations  14.2 us (8%)
    psum x1, waiting for transfers between devices, local_step(): projected = lax.psum(part_sum, 'tp')  57.5 us
    select_n x1, other arithmetic, local_step(): key_new = jnp.where(at_slot, key_val[:, None, :head_dim], k_cache)  17.4 us
    psum x1, waiting for transfers between devices, local_step(): lax.psum(jnp.einsum('bnt,btd->bnd', weights.astype(jnp.bfloat16), val_new...  16.6 us
    pmax x1, blocking collectives, local_step(): global_max = lax.pmax(local_max, 'sq')  14.8 us
    psum x1, blocking collectives, local_step(): denominator = lax.psum(jnp.sum(weights, axis=-1, keepdims=True), 'sq')  14.6 us
    dot_general x1, matrix products, local_step(): jnp.einsum('bnt,btd->bnd', weights.astype(jnp.bfloat16), val_new, preferr...  9.14 us
    dot_general x1, matrix products, local_step(): jnp.einsum('bnd,btd->bnt', query, key_new, preferred_element_type=jnp.flo...  8.14 us
    dot_general x1, matrix products, local_step(): part_sum = jnp.dot(attended, w_out, preferred_element_type=jnp.float32)  4.74 us
  transfers between devices with their start and end apart: 2, of which 2 were waited for; matrix products, arithmetic and copies ran while one was open for 1% of the time, Pallas kernels for 0%

commit v1 on v0

v1 whole, which is shorter than its diff:
```python
import functools
import jax
import jax.numpy as jnp
from jax import lax
from jax.experimental import pallas as pl
from jax.experimental.pallas import tpu as pltpu
from jax.sharding import PartitionSpec as P

MESH = pl.DeviceIdType.MESH
F32, BF16 = jnp.float32, jnp.bfloat16
CHUNK = 8
SLOTS = 24
LEAD = 16
HEAD = 128
LANES = 128


def attend_kernel(seqs, lens, x_hbm, kc, vc, gain, bias, wq_hbm, bq, wkv_hbm, bkv, kn, vn, num, stat,
                  x_s, h_s, wq_s, wkv_s, q_s, kv_s, kbuf, vbuf, sem_in, rk, rv, wk, wv):
    pos = kc.shape[1]
    heads = q_s.shape[1]
    chunks = seqs // CHUNK
    me = lax.axis_index("sq")
    base = me * pos

    def read(i):
        s = lax.rem(i, SLOTS)
        rows = pl.ds(i * CHUNK, CHUNK)
        return (pltpu.make_async_copy(kc.at[rows], kbuf.at[s], rk.at[s]),
                pltpu.make_async_copy(vc.at[rows], vbuf.at[s], rv.at[s]))

    def write(i):
        s = lax.rem(i, SLOTS)
        rows = pl.ds(i * CHUNK, CHUNK)
        return (pltpu.make_async_copy(kbuf.at[s], kn.at[rows], wk.at[s]),
                pltpu.make_async_copy(vbuf.at[s], vn.at[rows], wv.at[s]))

    parts = wq_hbm.shape[1] // 256
    in_x = pltpu.make_async_copy(x_hbm, x_s, sem_in.at[0])
    in_kv = pltpu.make_async_copy(wkv_hbm, wkv_s, sem_in.at[1])
    in_q = [pltpu.make_async_copy(wq_hbm.at[:, pl.ds(g * 256, 256)], wq_s.at[:, pl.ds(g * 256, 256)], sem_in.at[2 + g])
            for g in range(parts)]
    in_x.start()
    in_kv.start()
    for c in in_q:
        c.start()

    @pl.loop(0, LEAD)
    def _(i):
        for c in read(i):
            c.start()

    in_x.wait()
    rows_n = 32

    @pl.loop(0, x_s.shape[0] // rows_n)
    def _(r):
        rows = pl.ds(r * rows_n, rows_n)
        wide = x_s[rows, :].astype(F32)
        mean = jnp.mean(wide, axis=-1, keepdims=True)
        cent = wide - mean
        var = jnp.mean(cent * cent, axis=-1, keepdims=True)
        h_s[rows, :] = (cent * lax.rsqrt(var + 1e-5) * gain[...] + bias[...]).astype(BF16)

    in_kv.wait()
    kv_s[...] = (jnp.dot(h_s[...], wkv_s[...], preferred_element_type=F32) + bkv[...]).astype(BF16).astype(F32)
    for g in range(parts):
        in_q[g].wait()
        cols = slice(g * 256, (g + 1) * 256)
        q = (jnp.dot(h_s[...], wq_s[:, cols], preferred_element_type=F32) + bq[:, cols]).astype(BF16).astype(F32)
        q_s[:, 2 * g, :] = q[:, :HEAD]
        q_s[:, 2 * g + 1, :] = q[:, HEAD:]

    spot = lax.broadcasted_iota(jnp.int32, (heads, pos), 1) + base
    lane = lax.broadcasted_iota(jnp.int32, (heads, LANES), 1)
    row16 = lax.broadcasted_iota(jnp.int32, (16, HEAD), 0)
    stat[...] = jnp.zeros_like(stat)
    own = seqs // 4

    @pl.loop(0, chunks)
    def _(i):
        s = lax.rem(i, SLOTS)
        for c in read(i):
            c.wait()
        first = i * CHUNK
        for j in range(CHUNK):
            b = first + j
            slot = lens[b] - base
            inside = jnp.logical_and(slot >= 0, slot < pos)
            at = pl.multiple_of(jnp.where(inside, slot // 16, 0) * 16, 16)
            mark = row16 == jnp.where(inside, slot - at, -1)
            win = pl.ds(at, 16)
            new = kv_s[pl.ds(b, 1), :].astype(BF16)
            kbuf[s, j, win, :] = jnp.where(mark, new[:, :HEAD], kbuf[s, j, win, :])
            vbuf[s, j, win, :] = jnp.where(mark, new[:, HEAD:], vbuf[s, j, win, :])
        group = first // own
        off = first - group * own
        tops, sums = stat[group, 0], stat[group, 1]
        for j in range(CHUNK):
            b = first + j
            q = q_s[b].astype(BF16)
            sc = lax.dot_general(q, kbuf[s, j], (((1,), (1,)), ((), ())), preferred_element_type=F32) * (HEAD ** -0.5)
            valid = spot <= lens[b]
            sc = jnp.where(valid, sc, -1e30)
            top = jnp.max(sc, axis=1, keepdims=True)
            w = jnp.where(valid, jnp.exp(sc - top), 0.0)
            tot = jnp.sum(w, axis=1, keepdims=True)
            num[b] = jnp.dot(w.astype(BF16), vbuf[s, j], preferred_element_type=F32)
            tops = jnp.where(lane == off + j, top, tops)
            sums = jnp.where(lane == off + j, tot, sums)
        stat[group, 0] = tops
        stat[group, 1] = sums
        for c in write(i):
            c.start()
        ahead = i + LEAD

        @pl.when(ahead < chunks)
        def _():
            @pl.when(ahead >= SLOTS)
            def _():
                for c in write(ahead - SLOTS):
                    c.wait()
            for c in read(ahead):
                c.start()

    @pl.loop(max(0, chunks - SLOTS), chunks)
    def _(i):
        for c in write(i):
            c.wait()


def attend(lens, x, kc, vc, gain, bias, wq, bq, wkv, bkv):
    seqs, pos, _ = kc.shape
    heads = wq.shape[1] // HEAD
    width = x.shape[1]
    hbm = pl.BlockSpec(memory_space=pl.ANY)
    vmem = pl.BlockSpec(memory_space=pltpu.VMEM)
    smem = pl.BlockSpec(memory_space=pltpu.SMEM)
    return pl.pallas_call(
        functools.partial(attend_kernel, seqs),
        out_shape=(jax.ShapeDtypeStruct(kc.shape, BF16), jax.ShapeDtypeStruct(vc.shape, BF16),
                   jax.ShapeDtypeStruct((seqs, heads, HEAD), F32), jax.ShapeDtypeStruct((4, 2, heads, LANES), F32)),
        in_specs=[smem, hbm, hbm, hbm, vmem, vmem, hbm, vmem, hbm, vmem],
        out_specs=(hbm, hbm, vmem, vmem),
        scratch_shapes=[
            pltpu.VMEM((seqs, width), BF16), pltpu.VMEM((seqs, width), BF16), pltpu.VMEM(wq.shape, BF16),
            pltpu.VMEM(wkv.shape, BF16), pltpu.VMEM((seqs, heads, HEAD), F32), pltpu.VMEM((seqs, 2 * HEAD), F32),
            pltpu.VMEM((SLOTS, CHUNK, pos, HEAD), BF16), pltpu.VMEM((SLOTS, CHUNK, pos, HEAD), BF16),
            pltpu.SemaphoreType.DMA((8,)), pltpu.SemaphoreType.DMA((SLOTS,)), pltpu.SemaphoreType.DMA((SLOTS,)),
            pltpu.SemaphoreType.DMA((SLOTS,)), pltpu.SemaphoreType.DMA((SLOTS,)),
        ],
        compiler_params=pltpu.CompilerParams(vmem_limit_bytes=60 * 1024 * 1024),
        name="attend",
    )(lens, x, kc, vc, gain[None], bias[None], wq, bq[None], wkv, bkv[None])


def solution(mesh):
    def local_step(hidden, cache_lens, k_cache, v_cache, ln_gain, ln_bias, w_query, b_query, w_kv, b_kv, w_out, b_out):
        key_new, val_new, num, stat = attend(cache_lens, hidden, k_cache, v_cache, ln_gain, ln_bias, w_query, b_query, w_kv, b_kv)
        seqs, heads, _ = num.shape
        own = seqs // 4
        tops = stat[:, 0, :, :own].transpose(0, 2, 1).reshape(seqs, heads, 1)
        sums = stat[:, 1, :, :own].transpose(0, 2, 1).reshape(seqs, heads, 1)
        best = lax.pmax(tops, "sq")
        scale = jnp.exp(tops - best)
        den = lax.psum(sums * scale, "sq")
        full = lax.psum(num * scale, "sq")
        attended = (full / den).astype(BF16).reshape(seqs, heads * HEAD)
        projected = lax.psum(jnp.dot(attended, w_out, preferred_element_type=F32), "tp")
        out = (hidden.astype(F32) + projected + b_out).astype(BF16)
        return out, key_new, val_new

    cache_spec = P("dp", "sq", None)
    row_spec = P("dp", None)
    in_specs = (row_spec, P("dp"), cache_spec, cache_spec, P(None), P(None), P(None, "tp"), P("tp"), P(None, None), P(None), P("tp", None), P(None))
    out_specs = (row_spec, cache_spec, cache_spec)
    return jax.shard_map(local_step, mesh=mesh, in_specs=in_specs, out_specs=out_specs, check_vma=False)
```

time: 174 us -> 201 us (1.16)
  Pallas kernels: 0 us -> 76.1 us
  matrix products: 28.2 us -> 4.82 us
  other arithmetic: 27.3 us -> 7 us
  blocking collectives: 29.5 us -> 14.9 us
  waiting for transfers between devices: 74.1 us -> 82.5 us
    pallas_call x0 -> x1, Pallas kernels: none -> 76.1 us  [attend(): pl.pallas_call(functools.partial(attend_kernel, seqs), out_shape=(jax.Sha...]
    dot_general x5 -> x1, matrix products: 28.2 us -> 4.82 us  [local_step(): jnp.dot(attended, w_out, preferred_element_type=F32)]
    select_n x1 -> x0, other arithmetic: 17.4 us -> none  [local_step(): key_new = jnp.where(at_slot, key_val[:, None, :head_dim], k_cache)]
    psum x1, blocking collectives: 14.6 us -> 6.04 us  [local_step(): den = lax.psum(sums * scale, 'sq')]
    psum x2, waiting for transfers between devices: 74.1 us -> 82.4 us  [the longest x1 57.5 us: local_step(): lax.psum(jnp.dot(attended, w_out, preferred_element_type=F32), 'tp')]
    pmax x1, blocking collectives: 14.8 us -> 8.87 us  [local_step(): best = lax.pmax(tops, 'sq')]
    reduce_sum x3 -> x0, other arithmetic: 5.29 us -> none  [the longest x1 2.4 us: layer_norm(): variance = jnp.mean(centered * centered, axis=-1, keepdims=True)]
    mul x0 -> x1, other arithmetic: none -> 2.56 us  [local_step(): full = lax.psum(num * scale, 'sq')]
  transfers between devices with their start and end apart: 2 -> 2, of which waited for: 2 -> 2; matrix products, arithmetic and copies ran while one was open for 1% -> 0% of each run, Pallas kernels for 0% -> 0%
where the time goes in v1:
time: 201 us
  waiting for transfers between devices  82.5 us (41%)
  Pallas kernels  76.1 us (38%)
  blocking collectives  14.9 us (7%)
  between operations  14.1 us (7%)
  other arithmetic  7 us (3%)
  matrix products  4.82 us (2%)
    pallas_call x1, Pallas kernels, attend(): pl.pallas_call(functools.partial(attend_kernel, seqs), out_shape=(jax.Sha...  76.1 us
    psum x1, waiting for transfers between devices, local_step(): lax.psum(jnp.dot(attended, w_out, preferred_element_type=F32), 'tp')  57.5 us
    psum x1, waiting for transfers between devices, local_step(): full = lax.psum(num * scale, 'sq')  24.9 us
    pmax x1, blocking collectives, local_step(): best = lax.pmax(tops, 'sq')  8.87 us
    psum x1, blocking collectives, local_step(): den = lax.psum(sums * scale, 'sq')  6.04 us
    dot_general x1, matrix products, local_step(): jnp.dot(attended, w_out, preferred_element_type=F32)  4.82 us
  transfers between devices with their start and end apart: 2, of which 2 were waited for; matrix products, arithmetic and copies ran while one was open for 0% of the time, Pallas kernels for 0%

profile of v1, /device:TPU:0, one launch (start us, length us, event | category | flops | bytes accessed | tf_op | source)
XLA Modules:
  0.0 200.7 jit_solution(6310666167255851769)
XLA Ops:
  7.2 0.0 all-reduce.3.cloned.1.call-start
  7.2 76.1 %attend.1 = (bf16[256,256,128]{2,1,0:T(8,128)(2,1)}, bf16[256,256,128]{2,1,0:T(8,128)(2,1)}, f32[256,8,128]{2,1,0:T(8,128)}, f32[4,2,8,128]{3,2,1,0:T(8,128)}) custom-call(s32[256]{0:T(256)} %lens.1, bf16[256,2048]{1,0:T(8,128)(2,1)} %x_hbm.1, bf16[256,256,128]{2,1,0:T(8,128)(2,1)} %kc.1, bf16[256,256,128]{2,1,0:T(8,128)(2,1)} %vc.1, f32[1,2048]{1,0:T(1,128)} %bitcast.26, ...), custom_call_target="tpu_custom_call" | custom-call | tf_op jit(solution)/shard_map/attend/pallas_call | solution.py:139
  83.3 0.7 slice_bitcast_fusion
  84.1 0.1 reshape.17
  84.1 0.1 reshape.16
  84.2 8.9 %pmax.7 = f32[256,8,1]{0,1,2:T(8,128)S(1)} all-reduce(f32[256,8,1]{0,1,2:T(8,128)S(1)} %reshape.16), channel_id=1, replica_groups=mesh['dp'=1,'tp'=2,'sq'=4] {'sq'}, use_global_device_ids=true, to_apply=%region_0.0 | all-reduce | flops 2048 | bytes 16384 | tf_op jit(solution)/shard_map/pmax | solution.py:164
  93.1 0.1 copy.16
  93.3 2.6 %broadcast_multiply_fusion = f32[256,8,128]{2,1,0:T(8,128)} fusion(f32[256,8,128]{2,1,0:T(8,128)} %get-tuple-element.7, f32[256,8]{1,0:T(8,128)S(1)} %copy.16), kind=kLoop, calls=%fused_computation.5 | loop fusion | flops 262144 | bytes 2105344 | tf_op jit(solution)/shard_map/mul | solution.py:167
  95.8 0.0 all-reduce.3.cloned.1.call-update
  95.8 0.0 all-reduce.5.cloned.1.call-start
  95.9 6.0 %psum.22 = f32[256,8]{0,1:T(8,128)S(1)} all-reduce(f32[256,8]{0,1:T(8,128)S(1)} %get-tuple-element.13), channel_id=1, replica_groups=mesh['dp'=1,'tp'=2,'sq'=4] {'sq'}, use_global_device_ids=true, to_apply=%region_2.0 | all-reduce | flops 2048 | bytes 16384 | tf_op jit(solution)/shard_map/psum | solution.py:166
  101.9 0.1 copy.18
  102.1 24.9 %all-reduce.3.cloned.1.call-done = f32[256,8,128]{2,1,0:T(8,128)} async-done(((f32[256,8,128]{2,1,0:T(8,128)}), f32[256,8,128]{2,1,0:T(8,128)}) %all-reduce.3.cloned.1.call-update) | async-done | bytes 1048592 | tf_op jit(solution)/shard_map/psum | solution.py:167
  127.0 1.6 divide_convert_fusion
  128.6 0.0 copy-start
  128.6 0.0 copy-start.1
  128.6 4.8 %fusion = f32[256,2048]{1,0:T(8,128)} fusion(bf16[1024,2048]{1,0:T(8,128)(2,1)} %param.22, bf16[32,8,8,128]{3,2,1,0:T(8,128)(2,1)S(1)} %bitcast.25), kind=kOutput, calls=%fused_computation.2 | convolution fusion | flops 1073741824 | bytes 6815744 | tf_op jit(solution)/shard_map/dot_general | solution.py:169
  133.4 0.0 all-reduce.5.cloned.1.call-update
  133.4 57.5 %all-reduce.5.cloned.1.call-done = f32[256,2048]{1,0:T(8,128)} async-done(((f32[256,2048]{1,0:T(8,128)}), f32[256,2048]{1,0:T(8,128)}) %all-reduce.5.cloned.1.call-update) | async-done | bytes 2097168 | tf_op jit(solution)/shard_map/psum | solution.py:169
  191.0 0.0 copy-done
  191.0 0.0 copy-done.1
  191.0 2.9 %add_convert_fusion = bf16[256,2048]{1,0:T(8,128)(2,1)} fusion(f32[256,2048]{1,0:T(8,128)} %all-reduce.5.cloned.1.call-done, bf16[256,2048]{1,0:T(8,128)(2,1)S(1)} %copy-done, f32[2048]{0:T(1024)S(1)} %copy-done.1), kind=kLoop, calls=%fused_computation | loop fusion | flops 2097152 | bytes 4202496 | tf_op jit(solution)/shard_map/convert_element_type | solution.py:170
  (3 shorter events, 0.0 us)
Async XLA Ops:
  7.2 119.8 %all-reduce.3.cloned.1.call-start = ((), (), s32[]{:S(2)}) async-start(), calls=%async_computation | async-start | bytes 2097152 | tf_op jit(solution)/shard_map/psum | solution.py:167
  95.8 95.1 %all-reduce.5.cloned.1.call-start = ((), (), s32[]{:S(2)}) async-start(), calls=%async_computation.1 | async-start | bytes 4194304 | tf_op jit(solution)/shard_map/psum | solution.py:169
  128.6 62.4 %copy-start = (bf16[256,2048]{1,0:T(8,128)(2,1)S(1)}, bf16[256,2048]{1,0:T(8,128)(2,1)}, u32[]{:S(2)}) copy-start(bf16[256,2048]{1,0:T(8,128)(2,1)} %x_hbm.1) | copy-start | bytes 3145732
  128.6 62.4 %copy-start.1 = (f32[2048]{0:T(1024)S(1)}, f32[2048]{0:T(1024)}, u32[]{:S(2)}) copy-start(f32[2048]{0:T(1024)} %param.23) | copy-start | bytes 24580
Sparse Core Ops, SparseCore 0:
  96.0 30.9 all-reduce.2
  133.5 57.3 all-reduce.4

commit v2 on v1

v2 whole, which is shorter than its diff:
```python
import functools
import jax
import jax.numpy as jnp
from jax import lax
from jax.experimental import pallas as pl
from jax.experimental.pallas import tpu as pltpu
from jax.sharding import PartitionSpec as P

MESH = pl.DeviceIdType.MESH
F32, BF16 = jnp.float32, jnp.bfloat16
CHUNK = 16
SLOTS = 14
LEAD = 9
UNIT = 8
GROUPS = CHUNK // UNIT
HEAD = 128
LANES = 128


def attend_kernel(seqs, lens_hbm, x_hbm, kc, vc, gain_hbm, bias_hbm, wq_hbm, bq_hbm, wkv_hbm, bkv_hbm, kn, vn, part,
                  lens, gain, bias, bq, bkv, x_s, h_s, wq_s, wkv_s, q_s, kv_s, kbuf, vbuf, sem_in, rk, rv, wk, wv):
    pos = kc.shape[1]
    heads = q_s.shape[1]
    chunks = seqs // CHUNK
    me = lax.axis_index("sq")
    base = me * pos

    def read(i):
        s = lax.rem(i, SLOTS)
        rows = pl.ds(i * CHUNK, CHUNK)
        return (pltpu.make_async_copy(kc.at[rows], kbuf.at[s], rk.at[s]),
                pltpu.make_async_copy(vc.at[rows], vbuf.at[s], rv.at[s]))

    def write(i):
        s = lax.rem(i, SLOTS)
        rows = pl.ds(i * CHUNK, CHUNK)
        return (pltpu.make_async_copy(kbuf.at[s], kn.at[rows], wk.at[s]),
                pltpu.make_async_copy(vbuf.at[s], vn.at[rows], wv.at[s]))

    parts = wq_hbm.shape[1] // 256
    in_x = pltpu.make_async_copy(x_hbm, x_s, sem_in.at[0])
    in_kv = pltpu.make_async_copy(wkv_hbm, wkv_s, sem_in.at[1])
    in_q = [pltpu.make_async_copy(wq_hbm.at[:, pl.ds(g * 256, 256)], wq_s.at[:, pl.ds(g * 256, 256)], sem_in.at[2 + g])
            for g in range(parts)]
    small = [pltpu.make_async_copy(a, b, sem_in.at[8 + n])
             for n, (a, b) in enumerate(((gain_hbm, gain), (bias_hbm, bias), (bkv_hbm, bkv), (bq_hbm, bq), (lens_hbm, lens)))]
    in_x.start()
    for c in small:
        c.start()
    in_kv.start()
    for c in in_q:
        c.start()

    @pl.loop(0, LEAD)
    def _(i):
        for c in read(i):
            c.start()

    in_x.wait()
    for c in small:
        c.wait()
    rows_n = 32

    @pl.loop(0, x_s.shape[0] // rows_n)
    def _(r):
        rows = pl.ds(r * rows_n, rows_n)
        wide = x_s[rows, :].astype(F32)
        mean = jnp.mean(wide, axis=-1, keepdims=True)
        cent = wide - mean
        var = jnp.mean(cent * cent, axis=-1, keepdims=True)
        h_s[rows, :] = (cent * lax.rsqrt(var + 1e-5) * gain[...] + bias[...]).astype(BF16)

    in_kv.wait()
    kv_s[...] = (jnp.dot(h_s[...], wkv_s[...], preferred_element_type=F32) + bkv[...]).astype(BF16).astype(F32)
    for g in range(parts):
        in_q[g].wait()
        cols = slice(g * 256, (g + 1) * 256)
        q = (jnp.dot(h_s[...], wq_s[:, cols], preferred_element_type=F32) + bq[:, cols]).astype(BF16).astype(F32)
        q_s[:, 2 * g, :] = q[:, :HEAD]
        q_s[:, 2 * g + 1, :] = q[:, HEAD:]

    spot = lax.broadcasted_iota(jnp.int32, (heads, pos), 1) + base
    lane = lax.broadcasted_iota(jnp.int32, (heads, LANES), 1)
    row16 = lax.broadcasted_iota(jnp.int32, (16, HEAD), 0)
    def spread(i):
        return pl.multiple_of(i * CHUNK, CHUNK), lax.rem(i, SLOTS)

    def values(i, weights):
        first, s = spread(i)
        for j in range(CHUNK):
            part[i * GROUPS + j // UNIT, j % UNIT] = jnp.dot(weights[j], vbuf[s, j], preferred_element_type=F32)

    def body(i, weights):
        first, s = spread(i)
        for c in read(i):
            c.wait()
        for j in range(CHUNK):
            b = first + j
            slot = lens[b] - base
            inside = jnp.logical_and(slot >= 0, slot < pos)
            at = pl.multiple_of(jnp.where(inside, slot // 16, 0) * 16, 16)
            mark = row16 == jnp.where(inside, slot - at, -1)
            win = pl.ds(at, 16)
            new = kv_s[pl.ds(b, 1), :].astype(BF16)
            kbuf[s, j, win, :] = jnp.where(mark, new[:, :HEAD], kbuf[s, j, win, :])
            vbuf[s, j, win, :] = jnp.where(mark, new[:, HEAD:], vbuf[s, j, win, :])
        scores = [lax.dot_general(q_s[first + j].astype(BF16), kbuf[s, j], (((1,), (1,)), ((), ())), preferred_element_type=F32)
                  for j in range(CHUNK)]
        values(jnp.maximum(i - 1, 0), weights)
        out = []
        for g in range(GROUPS):
            stat = jnp.zeros((heads, LANES), F32)
            for j in range(UNIT):
                valid = spot <= lens[first + g * UNIT + j]
                sc = jnp.where(valid, scores[g * UNIT + j] * (HEAD ** -0.5), -1e30)
                top = jnp.max(sc, axis=1, keepdims=True)
                w = jnp.where(valid, jnp.exp(sc - top), 0.0)
                tot = jnp.sum(w, axis=1, keepdims=True)
                out.append(w.astype(BF16))
                stat = jnp.where(lane == j, top, jnp.where(lane == UNIT + j, tot, stat))
            part[i * GROUPS + g, UNIT] = stat
        for c in write(i):
            c.start()
        ahead = i + LEAD

        @pl.when(ahead < chunks)
        def _():
            @pl.when(ahead >= SLOTS)
            def _():
                for c in write(ahead - SLOTS):
                    c.wait()
            for c in read(ahead):
                c.start()

        return tuple(out)

    last = lax.fori_loop(0, chunks, body, tuple(jnp.zeros((heads, pos), BF16) for _ in range(CHUNK)))
    values(chunks - 1, last)

    @pl.loop(max(0, chunks - SLOTS), chunks)
    def _(i):
        for c in write(i):
            c.wait()


def attend(lens, x, kc, vc, gain, bias, wq, bq, wkv, bkv):
    seqs, pos, _ = kc.shape
    heads = wq.shape[1] // HEAD
    width = x.shape[1]
    hbm = pl.BlockSpec(memory_space=pltpu.HBM)
    vmem = pl.BlockSpec(memory_space=pltpu.VMEM)
    return pl.pallas_call(
        functools.partial(attend_kernel, seqs),
        out_shape=(jax.ShapeDtypeStruct(kc.shape, BF16), jax.ShapeDtypeStruct(vc.shape, BF16),
                   jax.ShapeDtypeStruct((seqs // UNIT, UNIT + 1, heads, HEAD), F32)),
        in_specs=[hbm] * 10,
        out_specs=(hbm, hbm, vmem),
        scratch_shapes=[
            pltpu.SMEM((seqs,), jnp.int32), pltpu.VMEM((1, width), F32), pltpu.VMEM((1, width), F32),
            pltpu.VMEM((1, wq.shape[1]), F32), pltpu.VMEM((1, 2 * HEAD), F32),
            pltpu.VMEM((seqs, width), BF16), pltpu.VMEM((seqs, width), BF16), pltpu.VMEM(wq.shape, BF16),
            pltpu.VMEM(wkv.shape, BF16), pltpu.VMEM((seqs, heads, HEAD), F32), pltpu.VMEM((seqs, 2 * HEAD), F32),
            pltpu.VMEM((SLOTS, CHUNK, pos, HEAD), BF16), pltpu.VMEM((SLOTS, CHUNK, pos, HEAD), BF16),
            pltpu.SemaphoreType.DMA((13,)), pltpu.SemaphoreType.DMA((SLOTS,)), pltpu.SemaphoreType.DMA((SLOTS,)),
            pltpu.SemaphoreType.DMA((SLOTS,)), pltpu.SemaphoreType.DMA((SLOTS,)),
        ],
        compiler_params=pltpu.CompilerParams(vmem_limit_bytes=44 * 1024 * 1024),
        name="attend",
    )(*(pltpu.with_memory_space_constraint(a, pltpu.HBM)
        for a in (lens, x, kc, vc, gain[None], bias[None], wq, bq[None], wkv, bkv[None])))


def merge_kernel(part, w_ref, x_ref, b_ref, out, near, mine, outbox, inbox, a_s, ys, yr, full, ss, rs):
    tp, sq = lax.axis_index("tp"), lax.axis_index("sq")
    mate = sq + 1 - 2 * lax.rem(sq, 2)
    across = lax.rem(sq + 2, 4)
    corner = 3 - sq
    units = part.shape[0] // 4
    rows = units * UNIT
    heads = part.shape[2]
    to_mate, to_across, to_twin = {"sq": mate}, {"sq": across}, {"tp": 1 - tp}
    lane = lax.broadcasted_iota(jnp.int32, (heads, LANES), 1)

    bar = pltpu.get_barrier_semaphore()
    for dev in (to_mate, to_across, to_twin):
        pl.semaphore_signal(bar, inc=1, device_id=dev, device_id_type=MESH)
    pl.semaphore_wait(bar, 3)

    def send(kind, k, src, dst, dev):
        return pltpu.make_async_remote_copy(src, dst, ss.at[kind, k], rs.at[kind, k], device_id=dev, device_id_type=MESH)

    def block(owner, k):
        return pl.ds(pl.multiple_of(owner * rows + k * UNIT, UNIT), UNIT)

    def c_near(k):
        return send(0, k, part.at[corner * units + k], near.at[k], to_mate)

    def c_mine(k):
        return send(1, k, part.at[mate * units + k], mine.at[k], to_mate)

    def c_cross(k):
        return send(2, k, outbox.at[k], inbox.at[k], to_across)

    def c_twin(k):
        r = pl.ds(k * UNIT, UNIT)
        return send(3, k, ys.at[r], yr.at[r], to_twin)

    def c_row(k):
        return send(4, k, full.at[block(sq, k)], full.at[block(sq, k)], to_across)

    def c_own(k):
        return send(5, k, full.at[block(sq, k)], full.at[block(sq, k)], to_mate)

    def c_pass(k):
        return send(6, k, full.at[block(across, k)], full.at[block(across, k)], to_mate)

    for k in range(units):
        c_near(k).start()
    for k in range(units):
        c_mine(k).start()

    def step_merge(k):
        c_near(k).wait_recv()
        own = across * units + k
        s0, s1 = part[own, UNIT], near[k, UNIT]
        top = jnp.maximum(s0, s1)
        e0, e1 = jnp.exp(s0 - top), jnp.exp(s1 - top)
        tot = pltpu.roll(s0, LANES - UNIT, 1) * e0 + pltpu.roll(s1, LANES - UNIT, 1) * e1
        for j in range(UNIT):
            outbox[k, j] = part[own, j] * e0[:, j:j + 1] + near[k, j] * e1[:, j:j + 1]
        outbox[k, UNIT] = jnp.where(lane < UNIT, top, jnp.where(lane < 2 * UNIT, pltpu.roll(tot, UNIT, 1), 0.0))
        c_cross(k).start()

    def step_combine(k):
        c_mine(k).wait_recv()
        c_cross(k).wait_recv()
        own = sq * units + k
        s0, s1, s2 = part[own, UNIT], mine[k, UNIT], inbox[k, UNIT]
        top = jnp.maximum(jnp.maximum(s0, s1), s2)
        e0, e1, e2 = jnp.exp(s0 - top), jnp.exp(s1 - top), jnp.exp(s2 - top)
        back = LANES - UNIT
        tot = pltpu.roll(s0, back, 1) * e0 + pltpu.roll(s1, back, 1) * e1 + pltpu.roll(s2, back, 1) * e2
        inv = 1.0 / jnp.where(lane < UNIT, tot, 1.0)
        e0, e1, e2 = e0 * inv, e1 * inv, e2 * inv
        for j in range(UNIT):
            a_s[k * UNIT + j] = part[own, j] * e0[:, j:j + 1] + mine[k, j] * e1[:, j:j + 1] + inbox[k, j] * e2[:, j:j + 1]

    def step_project(ks):
        r = pl.ds(ks[0] * UNIT, len(ks) * UNIT)
        lhs = jnp.concatenate([a_s[r, h, :].astype(BF16) for h in range(heads)], axis=1)
        ys[r, :] = jnp.dot(lhs, w_ref[...], preferred_element_type=F32)
        for k in ks:
            c_twin(k).start()

    def step_rows(k):
        c_twin(k).wait_recv()
        r = pl.ds(k * UNIT, UNIT)
        pair = x_ref[pl.ds(pl.multiple_of(sq * rows + (k // 2) * 2 * UNIT, 2 * UNIT), 2 * UNIT), :].astype(F32)
        half = pair[(k % 2) * UNIT:(k % 2 + 1) * UNIT]
        full[block(sq, k), :] = half + (ys[r, :] + yr[r, :]) + b_ref[...]
        c_row(k).start()
        c_own(k).start()

    def step_pass(k):
        c_row(k).wait_recv()
        c_pass(k).start()

    def step_store(owner, k2):
        r = pl.ds(pl.multiple_of(owner * rows + k2 * 2 * UNIT, 2 * UNIT), 2 * UNIT)
        out[r, :] = full[r, :].astype(BF16)

    for k in range(units):
        step_merge(k)
    for k in range(units):
        step_combine(k)
        step_project([k])
        if k >= 4:
            step_rows(k - 4)
        if k >= 6:
            step_pass(k - 6)
    for k in range(units - 4, units):
        step_rows(k)
        step_pass(k - 2)
    for k2 in range(units // 2):
        step_store(sq, k2)
    for k in range(units - 2, units):
        step_pass(k)
    for k2 in range(units // 2):
        step_store(across, k2)
    for k2 in range(units // 2):
        for k in (2 * k2, 2 * k2 + 1):
            c_own(k).wait_recv()
        step_store(mate, k2)
    for k2 in range(units // 2):
        for k in (2 * k2, 2 * k2 + 1):
            c_pass(k).wait_recv()
        step_store(corner, k2)
    for k in range(units):
        for c in (c_near, c_mine, c_cross, c_twin, c_row, c_own, c_pass):
            c(k).wait_send()


def merge(part, w_out, hidden, b_out):
    units = part.shape[0] // 4
    heads = part.shape[2]
    width = w_out.shape[1]
    rows = units * UNIT
    vmem = pl.BlockSpec(memory_space=pltpu.VMEM)
    box = pltpu.VMEM((units,) + part.shape[1:], F32)
    return pl.pallas_call(
        merge_kernel,
        out_shape=jax.ShapeDtypeStruct(hidden.shape, BF16),
        in_specs=[vmem] * 4,
        out_specs=vmem,
        scratch_shapes=[
            box, box, box, box, pltpu.VMEM((rows, heads, HEAD), F32), pltpu.VMEM((rows, width), F32), pltpu.VMEM((rows, width), F32),
            pltpu.VMEM((4 * rows, width), F32), pltpu.SemaphoreType.DMA((7, units)), pltpu.SemaphoreType.DMA((7, units)),
        ],
        compiler_params=pltpu.CompilerParams(collective_id=0, has_side_effects=True, vmem_limit_bytes=24 * 1024 * 1024),
        name="merge",
    )(part, w_out, hidden, b_out[None])


def solution(mesh):
    def local_step(hidden, cache_lens, k_cache, v_cache, ln_gain, ln_bias, w_query, b_query, w_kv, b_kv, w_out, b_out):
        key_new, val_new, part = attend(cache_lens, hidden, k_cache, v_cache, ln_gain, ln_bias, w_query, b_query, w_kv, b_kv)
        return merge(part, w_out, hidden, b_out), key_new, val_new

    cache_spec = P("dp", "sq", None)
    row_spec = P("dp", None)
    in_specs = (row_spec, P("dp"), cache_spec, cache_spec, P(None), P(None), P(None, "tp"), P("tp"), P(None, None), P(None), P("tp", None), P(None))
    out_specs = (row_spec, cache_spec, cache_spec)
    return jax.shard_map(local_step, mesh=mesh, in_specs=in_specs, out_specs=out_specs, check_vma=False)
```

time: 201 us -> 55.9 us (0.28)
  waiting for transfers between devices: 82.5 us -> 0 us
  Pallas kernels: 76.1 us -> 54.1 us
  blocking collectives: 14.9 us -> 0 us
  between operations: 14.1 us -> 0.7 us
  other arithmetic: 7 us -> 0 us
  matrix products: 4.82 us -> 0 us
    psum x2 -> x0, waiting for transfers between devices: 82.4 us -> none  [the longest x1 57.5 us: local_step(): lax.psum(jnp.dot(attended, w_out, preferred_element_type=F32), 'tp')]
    pallas_call x1, Pallas kernels: 76.1 us -> 26.2 us  [attend(): pl.pallas_call(functools.partial(attend_kernel, seqs), out_shape=(jax.Sha...]
    pallas_call x0 -> x1, Pallas kernels: none -> 27.9 us  [merge(): pl.pallas_call(merge_kernel, out_shape=jax.ShapeDtypeStruct(hidden.shape,...]
    pmax x1 -> x0, blocking collectives: 8.87 us -> none  [local_step(): best = lax.pmax(tops, 'sq')]
    psum x1 -> x0, blocking collectives: 6.04 us -> none  [local_step(): den = lax.psum(sums * scale, 'sq')]
    dot_general x1 -> x0, matrix products: 4.82 us -> none  [local_step(): jnp.dot(attended, w_out, preferred_element_type=F32)]
    convert_element_type x2 -> x0, other arithmetic: 4.43 us -> none  [the longest x1 2.87 us: local_step(): out = (hidden.astype(F32) + projected + b_out).astype(BF16)]
    mul x1 -> x0, other arithmetic: 2.56 us -> none  [local_step(): full = lax.psum(num * scale, 'sq')]
  transfers between devices with their start and end apart: 2 -> 0, of which waited for: 2 -> 0; matrix products, arithmetic and copies ran while one was open for 0% -> 0% of each run, Pallas kernels for 0% -> 0%
where the time goes in v2:
time: 55.9 us; the launch traced here: 55.8 us
  Pallas kernels  54.1 us (97%)
  local copies, waits for them, and re-layouts  0.99 us (2%)
  between operations  0.7 us (1%)
    pallas_call x1, Pallas kernels, merge(): pl.pallas_call(merge_kernel, out_shape=jax.ShapeDtypeStruct(hidden.shape,...  27.9 us
    pallas_call x1, Pallas kernels, attend(): pl.pallas_call(functools.partial(attend_kernel, seqs), out_shape=(jax.Sha...  26.2 us

profile of v2, /device:TPU:0, one launch (start us, length us, event | category | flops | bytes accessed | tf_op | source)
XLA Modules:
  0.0 55.8 jit_solution(10445632016932828520)
XLA Ops:
  0.6 0.0 copy-start
  0.6 0.0 copy-start.1
  0.7 0.0 copy-start.2
  0.7 26.2 %attend.1 = (bf16[256,256,128]{2,1,0:T(8,128)(2,1)}, bf16[256,256,128]{2,1,0:T(8,128)(2,1)}, f32[32,9,8,128]{3,2,1,0:T(8,128)S(1)}) custom-call(s32[256]{0:T(256)} %lens_hbm.1, bf16[256,2048]{1,0:T(8,128)(2,1)} %x_ref.1, bf16[256,256,128]{2,1,0:T(8,128)(2,1)} %kc.1, bf16[256,256,128]{2,1,0:T(8,128)(2,1)} %vc.1, f32[1,2048]{1,0:T(1,128)} %bitcast.6, ...), custom_call_target="tpu_custom_call" | custom-call | tf_op jit(solution)/shard_map/attend/pallas_call | solution.py:152
  26.9 0.0 copy-done
  26.9 0.0 copy-done.1
  26.9 0.0 copy-done.2
  26.9 27.9 %merge.1 = bf16[256,2048]{1,0:T(8,128)(2,1)S(1)} custom-call(f32[32,9,8,128]{3,2,1,0:T(8,128)S(1)} %get-tuple-element.6.part, bf16[1024,2048]{1,0:T(8,128)(2,1)S(1)} %copy-done, bf16[256,2048]{1,0:T(8,128)(2,1)S(1)} %copy-done.1, f32[1,2048]{1,0:T(1,128)S(1)} %bitcast.5), custom_call_target="tpu_custom_call" | custom-call | tf_op jit(solution)/shard_map/merge/pallas_call | solution.py:310
  54.8 1.0 %copy.16 = bf16[256,2048]{1,0:T(8,128)(2,1)} copy(bf16[256,2048]{1,0:T(8,128)(2,1)S(1)} %merge.1) | data formatting | bytes 2097152
Async XLA Ops:
  0.6 26.3 %copy-start = (bf16[1024,2048]{1,0:T(8,128)(2,1)S(1)}, bf16[1024,2048]{1,0:T(8,128)(2,1)}, u32[]{:S(2)}) copy-start(bf16[1024,2048]{1,0:T(8,128)(2,1)} %w_ref.1) | copy-start | bytes 12582916
  0.6 26.3 %copy-start.1 = (bf16[256,2048]{1,0:T(8,128)(2,1)S(1)}, bf16[256,2048]{1,0:T(8,128)(2,1)}, u32[]{:S(2)}) copy-start(bf16[256,2048]{1,0:T(8,128)(2,1)} %x_ref.1) | copy-start | bytes 3145732
  0.7 26.3 %copy-start.2 = (f32[2048]{0:T(1024)S(1)}, f32[2048]{0:T(1024)}, u32[]{:S(2)}) copy-start(f32[2048]{0:T(1024)} %param.23) | copy-start | bytes 24580

commit v3 on v2

--- a/solution.py
+++ b/solution.py
@@ -13,27 +13,31 @@
 LEAD = 9
 UNIT = 8
 GROUPS = CHUNK // UNIT
+EARLY = 3
 HEAD = 128
 LANES = 128
 
 
-def attend_kernel(seqs, lens_hbm, x_hbm, kc, vc, gain_hbm, bias_hbm, wq_hbm, bq_hbm, wkv_hbm, bkv_hbm, kn, vn, part,
-                  lens, gain, bias, bq, bkv, x_s, h_s, wq_s, wkv_s, q_s, kv_s, kbuf, vbuf, sem_in, rk, rv, wk, wv):
+def attend_kernel(seqs, lens_hbm, x_hbm, kc, vc, gain_hbm, bias_hbm, wq_hbm, bq_hbm, wkv_hbm, bkv_hbm, kn, vn, part, q_s, kv_s,
+                  lens, gain, bias, bq, bkv, x_s, h_s, wq_s, wkv_s, kbuf, vbuf, sem_in, rk, rv, wk, wv):
     pos = kc.shape[1]
     heads = q_s.shape[1]
-    chunks = seqs // CHUNK
+    chunks = 4 * EARLY
     me = lax.axis_index("sq")
     base = me * pos
 
+    def place(i):
+        return pl.multiple_of((i // EARLY) * (seqs // 4) + lax.rem(i, EARLY) * CHUNK, CHUNK)
+
     def read(i):
         s = lax.rem(i, SLOTS)
-        rows = pl.ds(i * CHUNK, CHUNK)
+        rows = pl.ds(place(i), CHUNK)
         return (pltpu.make_async_copy(kc.at[rows], kbuf.at[s], rk.at[s]),
                 pltpu.make_async_copy(vc.at[rows], vbuf.at[s], rv.at[s]))
 
     def write(i):
         s = lax.rem(i, SLOTS)
-        rows = pl.ds(i * CHUNK, CHUNK)
+        rows = pl.ds(place(i), CHUNK)
         return (pltpu.make_async_copy(kbuf.at[s], kn.at[rows], wk.at[s]),
                 pltpu.make_async_copy(vbuf.at[s], vn.at[rows], wv.at[s]))
 
@@ -51,7 +55,7 @@
     for c in in_q:
         c.start()
 
-    @pl.loop(0, LEAD)
+    @pl.loop(0, min(LEAD, chunks))
     def _(i):
         for c in read(i):
             c.start()
@@ -83,7 +87,7 @@
     lane = lax.broadcasted_iota(jnp.int32, (heads, LANES), 1)
     row16 = lax.broadcasted_iota(jnp.int32, (16, HEAD), 0)
     def spread(i):
-        return pl.multiple_of(i * CHUNK, CHUNK), lax.rem(i, SLOTS)
+        return place(i), lax.rem(i, SLOTS)
 
     def values(i, weights):
         first, s = spread(i)
@@ -152,14 +156,15 @@
     return pl.pallas_call(
         functools.partial(attend_kernel, seqs),
         out_shape=(jax.ShapeDtypeStruct(kc.shape, BF16), jax.ShapeDtypeStruct(vc.shape, BF16),
-                   jax.ShapeDtypeStruct((seqs // UNIT, UNIT + 1, heads, HEAD), F32)),
+                   jax.ShapeDtypeStruct((4 * EARLY * GROUPS, UNIT + 1, heads, HEAD), F32),
+                   jax.ShapeDtypeStruct((seqs, heads, HEAD), F32), jax.ShapeDtypeStruct((seqs, 2 * HEAD), F32)),
         in_specs=[hbm] * 10,
-        out_specs=(hbm, hbm, vmem),
+        out_specs=(hbm, hbm, vmem, vmem, vmem),
         scratch_shapes=[
             pltpu.SMEM((seqs,), jnp.int32), pltpu.VMEM((1, width), F32), pltpu.VMEM((1, width), F32),
             pltpu.VMEM((1, wq.shape[1]), F32), pltpu.VMEM((1, 2 * HEAD), F32),
             pltpu.VMEM((seqs, width), BF16), pltpu.VMEM((seqs, width), BF16), pltpu.VMEM(wq.shape, BF16),
-            pltpu.VMEM(wkv.shape, BF16), pltpu.VMEM((seqs, heads, HEAD), F32), pltpu.VMEM((seqs, 2 * HEAD), F32),
+            pltpu.VMEM(wkv.shape, BF16),
             pltpu.VMEM((SLOTS, CHUNK, pos, HEAD), BF16), pltpu.VMEM((SLOTS, CHUNK, pos, HEAD), BF16),
             pltpu.SemaphoreType.DMA((13,)), pltpu.SemaphoreType.DMA((SLOTS,)), pltpu.SemaphoreType.DMA((SLOTS,)),
             pltpu.SemaphoreType.DMA((SLOTS,)), pltpu.SemaphoreType.DMA((SLOTS,)),
@@ -170,14 +175,49 @@
         for a in (lens, x, kc, vc, gain[None], bias[None], wq, bq[None], wkv, bkv[None])))
 
 
-def merge_kernel(part, w_ref, x_ref, b_ref, out, near, mine, outbox, inbox, a_s, ys, yr, full, ss, rs):
+PLAN = {
+    3: [("merge", 0), ("merge", 1), ("merge", 2), ("merge", 3), ("merge", 4), ("merge", 5), ("attend", (6, 0)), ("attend", (6, 1)),
+        ("project", [0]), ("attend", (7, 0)), ("project", [1, 2]), ("attend", (7, 1)), ("values", 0), ("merge", 6), ("project", [3, 4]),
+        ("merge", 7), ("rows", 0), ("rows", 1), ("project", [5, 6]), ("rows", 2), ("rows", 3), ("project", [7]), ("pass", 0),
+        ("rows", 4), ("pass", 1), ("rows", 5), ("pass", 2), ("rows", 6), ("pass", 3), ("rows", 7), ("pass", 4), ("store", 0),
+        ("pass", 5), ("pass", 6), ("pass", 7), ("store", 1)],
+    2: [("attend", (4, 0)), ("merge", 0), ("merge", 1), ("merge", 2), ("merge", 3), ("attend", (4, 1)), ("attend", (5, 0)), ("merge", 4),
+        ("project", [0]), ("attend", (5, 1)), ("project", [1, 2]), ("attend", (6, 0)), ("merge", 5), ("rows", 0), ("attend", (6, 1)),
+        ("project", [3, 4]), ("attend", (7, 0)), ("merge", 6), ("rows", 1), ("attend", (7, 1)), ("values", 0), ("rows", 2), ("project", [5]),
+        ("merge", 7), ("rows", 3), ("project", [6]), ("pass", 0), ("rows", 4), ("pass", 1), ("project", [7]), ("pass", 2), ("rows", 5),
+        ("pass", 3), ("rows", 6), ("pass", 4), ("rows", 7), ("store", 0), ("pass", 5), ("pass", 6), ("pass", 7), ("store", 1)],
+}
+
+
+def merge_kernel(part, q_ref, kv_ref, kc, vc, lens_hbm, w_ref, x_ref, b_ref, out, k2, v2,
+                 lens, part2, near, mine, outbox, inbox, a_s, ys, yr, full, ss, rs, kr, vr, ls):
     tp, sq = lax.axis_index("tp"), lax.axis_index("sq")
     mate = sq + 1 - 2 * lax.rem(sq, 2)
     across = lax.rem(sq + 2, 4)
     corner = 3 - sq
-    units = part.shape[0] // 4
-    rows = units * UNIT
+    rows = x_ref.shape[0] // 4
+    units = rows // UNIT
+    early = part.shape[0] // 4
+    late = units - early
     heads = part.shape[2]
+    pos = kc.shape[1]
+    base = sq * pos
+
+    get_lens = pltpu.make_async_copy(lens_hbm, lens, ls.at[0])
+    get_lens.start()
+
+    def fetch(o, k):
+        src, dst, n = pl.ds(o * rows + k * UNIT, UNIT), pl.ds((o * late + k - early) * UNIT, UNIT), o * late + k - early
+        return (pltpu.make_async_copy(kc.at[src], k2.at[dst], kr.at[n]), pltpu.make_async_copy(vc.at[src], v2.at[dst], vr.at[n]))
+
+    for k in range(early, units):
+        for o in range(4):
+            for c in fetch(o, k):
+                c.start()
+
+    def piece(o, k):
+        return part.at[o * early + k] if k < early else part2.at[o * late + k - early]
+
     to_mate, to_across, to_twin = {"sq": mate}, {"sq": across}, {"tp": 1 - tp}
     lane = lax.broadcasted_iota(jnp.int32, (heads, LANES), 1)
 
@@ -193,10 +233,10 @@
         return pl.ds(pl.multiple_of(owner * rows + k * UNIT, UNIT), UNIT)
 
     def c_near(k):
-        return send(0, k, part.at[corner * units + k], near.at[k], to_mate)
+        return send(0, k, piece(corner, k), near.at[k], to_mate)
 
     def c_mine(k):
-        return send(1, k, part.at[mate * units + k], mine.at[k], to_mate)
+        return send(1, k, piece(mate, k), mine.at[k], to_mate)
 
     def c_cross(k):
         return send(2, k, outbox.at[k], inbox.at[k], to_across)
@@ -214,28 +254,65 @@
     def c_pass(k):
         return send(6, k, full.at[block(across, k)], full.at[block(across, k)], to_mate)
 
-    for k in range(units):
+    def step_near(k):
         c_near(k).start()
-    for k in range(units):
         c_mine(k).start()
+
+    spot = lax.broadcasted_iota(jnp.int32, (heads, pos), 1)
+
+    def step_values(k, pair, weights):
+        for n, o in enumerate(pair):
+            dst = piece(o, k)
+            for j in range(UNIT):
+                w, extra = weights[n * UNIT + j]
+                dst[j] = jnp.dot(w, v2[(o * late + k - early) * UNIT + j], preferred_element_type=F32) + extra
+
+    def step_attend(k, pair, before):
+        for o in pair:
+            for c in fetch(o, k):
+                c.wait()
+        where = [(o, o * rows + k * UNIT + j, (o * late + k - early) * UNIT + j) for o in pair for j in range(UNIT)]
+        scores = [lax.dot_general(q_ref[b].astype(BF16), k2[n], (((1,), (1,)), ((), ())), preferred_element_type=F32)
+                  for _, b, n in where]
+        if before is not None:
+            step_values(*before)
+        weights = []
+        stats = {o: jnp.zeros((heads, LANES), F32) for o in pair}
+        for (o, b, _), sc in zip(where, scores):
+            j = b % UNIT
+            at = lens[b] - base
+            new = kv_ref[b:b + 1, :]
+            fresh = jnp.sum(q_ref[b] * new[:, :HEAD], axis=1, keepdims=True)
+            here = spot == at
+            sc = jnp.where(spot <= at, jnp.where(here, fresh, sc) * (HEAD ** -0.5), -1e30)
+            top = jnp.max(sc, axis=1, keepdims=True)
+            w = jnp.where(spot <= at, jnp.exp(sc - top), 0.0)
+            tot = jnp.sum(w, axis=1, keepdims=True)
+            mine_w = jnp.sum(jnp.where(here, w, 0.0), axis=1, keepdims=True)
+            extra = mine_w.astype(BF16).astype(F32) * new[:, HEAD:]
+            weights.append((jnp.where(here, 0.0, w).astype(BF16), extra))
+            stats[o] = jnp.where(lane == j, top, jnp.where(lane == UNIT + j, tot, stats[o]))
+        for o in pair:
+            piece(o, k)[UNIT] = stats[o]
+        return (k, pair, weights)
 
     def step_merge(k):
         c_near(k).wait_recv()
-        own = across * units + k
-        s0, s1 = part[own, UNIT], near[k, UNIT]
+        own = piece(across, k)
+        s0, s1 = own[UNIT], near[k, UNIT]
         top = jnp.maximum(s0, s1)
         e0, e1 = jnp.exp(s0 - top), jnp.exp(s1 - top)
         tot = pltpu.roll(s0, LANES - UNIT, 1) * e0 + pltpu.roll(s1, LANES - UNIT, 1) * e1
         for j in range(UNIT):
-            outbox[k, j] = part[own, j] * e0[:, j:j + 1] + near[k, j] * e1[:, j:j + 1]
+            outbox[k, j] = own[j] * e0[:, j:j + 1] + near[k, j] * e1[:, j:j + 1]
         outbox[k, UNIT] = jnp.where(lane < UNIT, top, jnp.where(lane < 2 * UNIT, pltpu.roll(tot, UNIT, 1), 0.0))
         c_cross(k).start()
 
     def step_combine(k):
         c_mine(k).wait_recv()
         c_cross(k).wait_recv()
-        own = sq * units + k
-        s0, s1, s2 = part[own, UNIT], mine[k, UNIT], inbox[k, UNIT]
+        own = piece(sq, k)
+        s0, s1, s2 = own[UNIT], mine[k, UNIT], inbox[k, UNIT]
         top = jnp.maximum(jnp.maximum(s0, s1), s2)
         e0, e1, e2 = jnp.exp(s0 - top), jnp.exp(s1 - top), jnp.exp(s2 - top)
         back = LANES - UNIT
@@ -243,7 +320,7 @@
         inv = 1.0 / jnp.where(lane < UNIT, tot, 1.0)
         e0, e1, e2 = e0 * inv, e1 * inv, e2 * inv
         for j in range(UNIT):
-            a_s[k * UNIT + j] = part[own, j] * e0[:, j:j + 1] + mine[k, j] * e1[:, j:j + 1] + inbox[k, j] * e2[:, j:j + 1]
+            a_s[k * UNIT + j] = own[j] * e0[:, j:j + 1] + mine[k, j] * e1[:, j:j + 1] + inbox[k, j] * e2[:, j:j + 1]
 
     def step_project(ks):
         r = pl.ds(ks[0] * UNIT, len(ks) * UNIT)
@@ -269,62 +346,131 @@
         r = pl.ds(pl.multiple_of(owner * rows + k2 * 2 * UNIT, 2 * UNIT), 2 * UNIT)
         out[r, :] = full[r, :].astype(BF16)
 
-    for k in range(units):
-        step_merge(k)
-    for k in range(units):
-        step_combine(k)
-        step_project([k])
-        if k >= 4:
-            step_rows(k - 4)
-        if k >= 6:
-            step_pass(k - 6)
-    for k in range(units - 4, units):
-        step_rows(k)
-        step_pass(k - 2)
-    for k2 in range(units // 2):
-        step_store(sq, k2)
-    for k in range(units - 2, units):
-        step_pass(k)
-    for k2 in range(units // 2):
-        step_store(across, k2)
-    for k2 in range(units // 2):
-        for k in (2 * k2, 2 * k2 + 1):
+    for k in range(early):
+        step_near(k)
+    get_lens.wait()
+    plan = PLAN[EARLY]
+    before = None
+    for name, k in plan:
+        if name == "attend":
+            k, half = k
+            before = step_attend(k, ((0, 1), (2, 3))[half], before)
+            if half == 0 and k > early:
+                step_near(k - 1)
+        elif name == "values":
+            step_values(*before)
+            step_near(units - 1)
+        elif name == "merge":
+            step_merge(k)
+        elif name == "project":
+            for n in k:
+                step_combine(n)
+            step_project(k)
+        elif name == "rows":
+            step_rows(k)
+        elif name == "pass":
+            step_pass(k)
+        elif name == "store":
+            for n in range(units // 2):
+                step_store((sq, across)[k], n)
+    for n in range(units // 2):
+        for k in (2 * n, 2 * n + 1):
             c_own(k).wait_recv()
-        step_store(mate, k2)
-    for k2 in range(units // 2):
-        for k in (2 * k2, 2 * k2 + 1):
+        step_store(mate, n)
+    for n in range(units // 2):
+        for k in (2 * n, 2 * n + 1):
             c_pass(k).wait_recv()
-        step_store(corner, k2)
+        step_store(corner, n)
     for k in range(units):
         for c in (c_near, c_mine, c_cross, c_twin, c_row, c_own, c_pass):
             c(k).wait_send()
 
 
-def merge(part, w_out, hidden, b_out):
-    units = part.shape[0] // 4
+def merge(part, q, kv, kc, vc, lens, w_out, hidden, b_out):
     heads = part.shape[2]
-    width = w_out.shape[1]
-    rows = units * UNIT
+    seqs, width = hidden.shape
+    rows = seqs // 4
+    units = rows // UNIT
+    left = seqs - 4 * EARLY * CHUNK
     vmem = pl.BlockSpec(memory_space=pltpu.VMEM)
+    hbm = pl.BlockSpec(memory_space=pltpu.HBM)
     box = pltpu.VMEM((units,) + part.shape[1:], F32)
+    pin = lambda a: pltpu.with_memory_space_constraint(a, pltpu.HBM)
+    kept = pltpu.VMEM((left,) + kc.shape[1:], BF16)
     return pl.pallas_call(
         merge_kernel,
-        out_shape=jax.ShapeDtypeStruct(hidden.shape, BF16),
-        in_specs=[vmem] * 4,
-        out_specs=vmem,
+        out_shape=(jax.ShapeDtypeStruct(hidden.shape, BF16), kept, kept),
+        in_specs=[vmem, vmem, vmem, hbm, hbm, hbm, vmem, vmem, vmem],
+        out_specs=(vmem, vmem, vmem),
         scratch_shapes=[
+            pltpu.SMEM((seqs,), jnp.int32), pltpu.VMEM((left // UNIT,) + part.shape[1:], F32),
             box, box, box, box, pltpu.VMEM((rows, heads, HEAD), F32), pltpu.VMEM((rows, width), F32), pltpu.VMEM((rows, width), F32),
             pltpu.VMEM((4 * rows, width), F32), pltpu.SemaphoreType.DMA((7, units)), pltpu.SemaphoreType.DMA((7, units)),
+            pltpu.SemaphoreType.DMA((left // UNIT,)), pltpu.SemaphoreType.DMA((left // UNIT,)), pltpu.SemaphoreType.DMA((1,)),
         ],
-        compiler_params=pltpu.CompilerParams(collective_id=0, has_side_effects=True, vmem_limit_bytes=24 * 1024 * 1024),
+        compiler_params=pltpu.CompilerParams(collective_id=0, has_side_effects=True, vmem_limit_bytes=16 * 1024 * 1024),
         name="merge",
-    )(part, w_out, hidden, b_out[None])
+    )(part, q, kv, pin(kc), pin(vc), pin(lens), w_out, hidden, b_out[None])
+
+
+def store_kernel(kv, lens_hbm, y, k2_in, v2_in, kn_in, vn_in, kn, vn, y_out, k2, v2, lens, sem, wk, wv):
+    del k2_in, v2_in, kn_in, vn_in
+    seqs, pos = kn.shape[:2]
+    own = seqs // 4
+    left = k2.shape[0] // 4
+    base = lax.axis_index("sq") * pos
+    row16 = lax.broadcasted_iota(jnp.int32, (16, HEAD), 0)
+    get_lens = pltpu.make_async_copy(lens_hbm, lens, sem.at[0])
+    put_y = pltpu.make_async_copy(y, y_out, sem.at[1])
+    get_lens.start()
+    put_y.start()
+    get_lens.wait()
+    pieces = []
+    for o in range(4):
+        for n in range(left // CHUNK):
+            first, kept = o * own + own - left + n * CHUNK, o * left + n * CHUNK
+            for j in range(CHUNK):
+                b = first + j
+                slot = lens[b] - base
+                inside = jnp.logical_and(slot >= 0, slot < pos)
+                at = pl.multiple_of(jnp.where(inside, slot // 16, 0) * 16, 16)
+                mark = row16 == jnp.where(inside, slot - at, -1)
+                win = pl.ds(at, 16)
+                new = kv[b:b + 1, :].astype(BF16)
+                k2[kept + j, win, :] = jnp.where(mark, new[:, :HEAD], k2[kept + j, win, :])
+                v2[kept + j, win, :] = jnp.where(mark, new[:, HEAD:], v2[kept + j, win, :])
+            src, dst, m = pl.ds(kept, CHUNK), pl.ds(first, CHUNK), len(pieces) // 2
+            pieces += [pltpu.make_async_copy(k2.at[src], kn.at[dst], wk.at[m]), pltpu.make_async_copy(v2.at[src], vn.at[dst], wv.at[m])]
+            pieces[-2].start()
+            pieces[-1].start()
+    for c in pieces:
+        c.wait()
+    put_y.wait()
+
+
+def store(kv, lens, y, k2, v2, kn, vn):
+    vmem = pl.BlockSpec(memory_space=pltpu.VMEM)
+    hbm = pl.BlockSpec(memory_space=pltpu.HBM)
+    n = k2.shape[0] // CHUNK
+    kept = pltpu.VMEM(k2.shape, BF16)
+    return pl.pallas_call(
+        store_kernel,
+        out_shape=(jax.ShapeDtypeStruct(kn.shape, BF16), jax.ShapeDtypeStruct(vn.shape, BF16), jax.ShapeDtypeStruct(y.shape, BF16), kept, kept),
+        in_specs=[vmem, hbm, vmem, vmem, vmem, hbm, hbm],
+        out_specs=(hbm, hbm, hbm, vmem, vmem),
+        input_output_aliases={3: 3, 4: 4, 5: 0, 6: 1},
+        scratch_shapes=[pltpu.SMEM(lens.shape, jnp.int32), pltpu.SemaphoreType.DMA((2,)), pltpu.SemaphoreType.DMA((n,)), pltpu.SemaphoreType.DMA((n,))],
+        compiler_params=pltpu.CompilerParams(vmem_limit_bytes=4 * 1024 * 1024),
+        name="store",
+    )(kv, pltpu.with_memory_space_constraint(lens, pltpu.HBM), y, k2, v2, kn, vn)[:3]
 
 
 def solution(mesh):
     def local_step(hidden, cache_lens, k_cache, v_cache, ln_gain, ln_bias, w_query, b_query, w_kv, b_kv, w_out, b_out):
-        key_new, val_new, part = attend(cache_lens, hidden, k_cache, v_cache, ln_gain, ln_bias, w_query, b_query, w_kv, b_kv)
-        return merge(part, w_out, hidden, b_out), key_new, val_new
+        key_part, val_part, part, q, kv = attend(cache_lens, hidden, k_cache, v_cache, ln_gain, ln_bias, w_query, b_query, w_kv, b_kv)
+        y, k2, v2 = merge(part, q, kv, k_cache, v_cache, cache_lens, w_out, hidden, b_out)
+        key_new, val_new, out = store(kv, cache_lens, y, k2, v2, key_part, val_part)
+        return out, key_new, val_new
 
     cache_spec = P("dp", "sq", None)
     row_spec = P("dp", None)

time: 55.9 us -> 52.9 us (0.946)
  Pallas kernels: 54.1 us -> 52.1 us
  local copies, waits for them, and re-layouts: 0.99 us -> 0.01 us
    pallas_call x1, Pallas kernels: 26.2 us -> 20 us  [attend(): pl.pallas_call(functools.partial(attend_kernel, seqs), out_shape=(jax.Sha...]
    pallas_call x1 -> x2, Pallas kernels: 27.9 us -> 32.1 us  [the longest x1 27.9 us: merge(): pl.pallas_call(merge_kernel, out_shape=(jax.ShapeDtypeStruct(hidden.shape...]
    unnamed x7 -> x6, local copies, waits for them, and re-layouts: 0.99 us -> 0.01 us
where the time goes in v3:
time: 52.9 us; the launch traced here: 52.8 us
  Pallas kernels  52.1 us (98%)
  between operations  0.7 us (1%)
    pallas_call x1, Pallas kernels, merge(): pl.pallas_call(merge_kernel, out_shape=(jax.ShapeDtypeStruct(hidden.shape...  27.9 us
    pallas_call x1, Pallas kernels, attend(): pl.pallas_call(functools.partial(attend_kernel, seqs), out_shape=(jax.Sha...  20 us
    pallas_call x1, Pallas kernels, store(): pl.pallas_call(store_kernel, out_shape=(jax.ShapeDtypeStruct(kn.shape, BF...  4.18 us

profile of v3, /device:TPU:0, one launch (start us, length us, event | category | flops | bytes accessed | tf_op | source)
XLA Modules:
  0.0 52.8 jit_solution(838565765721904731)
XLA Ops:
  0.6 0.0 copy-start
  0.6 0.0 copy-start.1
  0.7 0.0 copy-start.2
  0.7 20.0 %attend.1 = (bf16[256,256,128]{2,1,0:T(8,128)(2,1)}, bf16[256,256,128]{2,1,0:T(8,128)(2,1)}, f32[24,9,8,128]{3,2,1,0:T(8,128)S(1)}, f32[256,8,128]{2,1,0:T(8,128)S(1)}, f32[256,256]{1,0:T(8,128)S(1)}) custom-call(s32[256]{0:T(256)} %lens_hbm.5, bf16[256,2048]{1,0:T(8,128)(2,1)} %x_ref.1, bf16[256,256,128]{2,1,0:T(8,128)(2,1)} %kc.3, ...), custom_call_target="tpu_custom_call" | custom-call | tf_op jit(solution)/shard_map/attend/pallas_call | solution.py:156
  20.7 0.0 copy-done
  20.7 0.0 copy-done.1
  20.7 0.0 copy-done.2
  20.7 27.9 %merge.1 = (bf16[256,2048]{1,0:T(8,128)(2,1)S(1)}, bf16[64,256,128]{2,1,0:T(8,128)(2,1)S(1)}, bf16[64,256,128]{2,1,0:T(8,128)(2,1)S(1)}) custom-call(f32[24,9,8,128]{3,2,1,0:T(8,128)S(1)} %get-tuple-element.15.part, f32[256,8,128]{2,1,0:T(8,128)S(1)} %get-tuple-element.16.q_ref, f32[256,256]{1,0:T(8,128)S(1)} %get-tuple-element.14.kv_ref.kv, ...), custom_call_target="tpu_custom_call" | custom-call | tf_op jit(solution)/shard_map/merge/pallas_call | solution.py:400
  48.7 4.2 %store.1 = (bf16[256,256,128]{2,1,0:T(8,128)(2,1)}, bf16[256,256,128]{2,1,0:T(8,128)(2,1)}, bf16[256,2048]{1,0:T(8,128)(2,1)}, bf16[64,256,128]{2,1,0:T(8,128)(2,1)S(1)}, bf16[64,256,128]{2,1,0:T(8,128)(2,1)S(1)}) custom-call(f32[256,256]{1,0:T(8,128)S(1)} %get-tuple-element.14.kv_ref.kv, ...), custom_call_target="tpu_custom_call", output_to_operand_aliasing={{3}: (3, {}), {4}: (4, {}), {0}: (5, {}), {1}: (6, {})} | custom-call | tf_op jit(solution)/shard_map/store/pallas_call | solution.py:456
Async XLA Ops:
  0.6 20.1 %copy-start = (bf16[256,2048]{1,0:T(8,128)(2,1)S(1)}, bf16[256,2048]{1,0:T(8,128)(2,1)}, u32[]{:S(2)}) copy-start(bf16[256,2048]{1,0:T(8,128)(2,1)} %x_ref.1) | copy-start | bytes 3145732
  0.6 20.1 %copy-start.1 = (bf16[1024,2048]{1,0:T(8,128)(2,1)S(1)}, bf16[1024,2048]{1,0:T(8,128)(2,1)}, u32[]{:S(2)}) copy-start(bf16[1024,2048]{1,0:T(8,128)(2,1)} %w_ref.1) | copy-start | bytes 12582916
  0.7 20.1 %copy-start.2 = (f32[2048]{0:T(1024)S(1)}, f32[2048]{0:T(1024)}, u32[]{:S(2)}) copy-start(f32[2048]{0:T(1024)} %param.23) | copy-start | bytes 24580

commit v4 on v3

--- a/solution.py
+++ b/solution.py
@@ -13,9 +13,19 @@
 LEAD = 9
 UNIT = 8
 GROUPS = CHUNK // UNIT
-EARLY = 3
+AHEAD = 3
+EARLY = 2
 HEAD = 128
 LANES = 128
+SHARED = 1
+PLAN = [
+    ("attend", (4, 0)), ("merge", 1), ("attend", (4, 1)), ("merge", 0), ("attend", (5, 0)), ("attend", (5, 1)), ("merge", 2),
+    ("merge", 3), ("merge", 4), ("attend", (6, 0)), ("project", [0, 1]), ("attend", (6, 1)), ("attend", (7, 0)),
+    ("merge", 5), ("attend", (7, 1)), ("merge", 6), ("values", 0), ("rows", 0), ("project", [2, 3]), ("rows", 1),
+    ("merge", 7), ("merge", 8), ("project", [4]), ("project", [5, 6]), ("rows", 2), ("rows", 3), ("project", [7]),
+    ("rows", 4), ("pass", 2), ("rows", 5), ("project", [8]), ("pass", 1), ("pass", 0), ("rows", 6), ("pass", 4), ("pass", 5),
+    ("pass", 3), ("rows", 8), ("rows", 7), ("pass", 6),
+]
 
 
 def attend_kernel(seqs, lens_hbm, x_hbm, kc, vc, gain_hbm, bias_hbm, wq_hbm, bq_hbm, wkv_hbm, bkv_hbm, kn, vn, part, q_s, kv_s,
@@ -175,90 +185,94 @@
         for a in (lens, x, kc, vc, gain[None], bias[None], wq, bq[None], wkv, bkv[None])))
 
 
-PLAN = {
-    3: [("merge", 0), ("merge", 1), ("merge", 2), ("merge", 3), ("merge", 4), ("merge", 5), ("attend", (6, 0)), ("attend", (6, 1)),
-        ("project", [0]), ("attend", (7, 0)), ("project", [1, 2]), ("attend", (7, 1)), ("values", 0), ("merge", 6), ("project", [3, 4]),
-        ("merge", 7), ("rows", 0), ("rows", 1), ("project", [5, 6]), ("rows", 2), ("rows", 3), ("project", [7]), ("pass", 0),
-        ("rows", 4), ("pass", 1), ("rows", 5), ("pass", 2), ("rows", 6), ("pass", 3), ("rows", 7), ("pass", 4), ("store", 0),
-        ("pass", 5), ("pass", 6), ("pass", 7), ("store", 1)],
-    2: [("attend", (4, 0)), ("merge", 0), ("merge", 1), ("merge", 2), ("merge", 3), ("attend", (4, 1)), ("attend", (5, 0)), ("merge", 4),
-        ("project", [0]), ("attend", (5, 1)), ("project", [1, 2]), ("attend", (6, 0)), ("merge", 5), ("rows", 0), ("attend", (6, 1)),
-        ("project", [3, 4]), ("attend", (7, 0)), ("merge", 6), ("rows", 1), ("attend", (7, 1)), ("values", 0), ("rows", 2), ("project", [5]),
-        ("merge", 7), ("rows", 3), ("project", [6]), ("pass", 0), ("rows", 4), ("pass", 1), ("project", [7]), ("pass", 2), ("rows", 5),
-        ("pass", 3), ("rows", 6), ("pass", 4), ("rows", 7), ("store", 0), ("pass", 5), ("pass", 6), ("pass", 7), ("store", 1)],
-}
-
-
-def merge_kernel(part, q_ref, kv_ref, kc, vc, lens_hbm, w_ref, x_ref, b_ref, out, k2, v2,
+def merge_kernel(part1, q_s, kv_s, kc, vc, lens_hbm, wo_s, x_s, bo, out, k2, v2,
                  lens, part2, near, mine, outbox, inbox, a_s, ys, yr, full, ss, rs, kr, vr, ls):
     tp, sq = lax.axis_index("tp"), lax.axis_index("sq")
-    mate = sq + 1 - 2 * lax.rem(sq, 2)
+    core = lax.rem(sq, 2)
+    mate = sq + 1 - 2 * core
     across = lax.rem(sq + 2, 4)
     corner = 3 - sq
-    rows = x_ref.shape[0] // 4
+    rows = x_s.shape[0] // 4
     units = rows // UNIT
-    early = part.shape[0] // 4
+    early = part1.shape[0] // 4
     late = units - early
-    heads = part.shape[2]
+    alone = units - SHARED
+    slots = alone + 2 * SHARED
+    heads = q_s.shape[1]
     pos = kc.shape[1]
     base = sq * pos
+    to_mate, to_across, to_twin = {"sq": mate}, {"sq": across}, {"tp": 1 - tp}
+    lane = lax.broadcasted_iota(jnp.int32, (heads, LANES), 1)
+    spot = lax.broadcasted_iota(jnp.int32, (heads, pos), 1)
 
     get_lens = pltpu.make_async_copy(lens_hbm, lens, ls.at[0])
     get_lens.start()
 
     def fetch(o, k):
-        src, dst, n = pl.ds(o * rows + k * UNIT, UNIT), pl.ds((o * late + k - early) * UNIT, UNIT), o * late + k - early
+        n = o * late + k - early
+        src, dst = pl.ds(o * rows + k * UNIT, UNIT), pl.ds(n * UNIT, UNIT)
         return (pltpu.make_async_copy(kc.at[src], k2.at[dst], kr.at[n]), pltpu.make_async_copy(vc.at[src], v2.at[dst], vr.at[n]))
 
-    for k in range(early, units):
-        for o in range(4):
-            for c in fetch(o, k):
-                c.start()
-
-    def piece(o, k):
-        return part.at[o * early + k] if k < early else part2.at[o * late + k - early]
-
-    to_mate, to_across, to_twin = {"sq": mate}, {"sq": across}, {"tp": 1 - tp}
-    lane = lax.broadcasted_iota(jnp.int32, (heads, LANES), 1)
+    halves = [(k, pair) for k in range(early, units) for pair in ((0, 1), (2, 3))]
+
+    def begin(n):
+        if n < len(halves):
+            for o in halves[n][1]:
+                for c in fetch(o, halves[n][0]):
+                    c.start()
+
+    for n in range(AHEAD):
+        begin(n)
 
     bar = pltpu.get_barrier_semaphore()
     for dev in (to_mate, to_across, to_twin):
         pl.semaphore_signal(bar, inc=1, device_id=dev, device_id_type=MESH)
     pl.semaphore_wait(bar, 3)
 
-    def send(kind, k, src, dst, dev):
-        return pltpu.make_async_remote_copy(src, dst, ss.at[kind, k], rs.at[kind, k], device_id=dev, device_id_type=MESH)
-
-    def block(owner, k):
-        return pl.ds(pl.multiple_of(owner * rows + k * UNIT, UNIT), UNIT)
-
-    def c_near(k):
-        return send(0, k, piece(corner, k), near.at[k], to_mate)
-
-    def c_mine(k):
-        return send(1, k, piece(mate, k), mine.at[k], to_mate)
-
-    def c_cross(k):
-        return send(2, k, outbox.at[k], inbox.at[k], to_across)
-
-    def c_twin(k):
-        r = pl.ds(k * UNIT, UNIT)
-        return send(3, k, ys.at[r], yr.at[r], to_twin)
-
-    def c_row(k):
-        return send(4, k, full.at[block(sq, k)], full.at[block(sq, k)], to_across)
-
-    def c_own(k):
-        return send(5, k, full.at[block(sq, k)], full.at[block(sq, k)], to_mate)
-
-    def c_pass(k):
-        return send(6, k, full.at[block(across, k)], full.at[block(across, k)], to_mate)
+    def send(kind, s, src, dst, dev):
+        return pltpu.make_async_remote_copy(src, dst, ss.at[kind, s], rs.at[kind, s], device_id=dev, device_id_type=MESH)
+
+    def unit_of(s):
+        return s if s < alone else alone + (s - alone) % SHARED
+
+    def owner_of(s, which):
+        return which if s < alone else lax.rem(which, 2) + 2 * ((s - alone) // SHARED)
+
+    def piece(o, k):
+        return part1.at[o * early + k] if k < early else part2.at[o * late + k - early]
+
+    def block(o, k):
+        return pl.ds(pl.multiple_of(o * rows + k * UNIT, UNIT), UNIT)
+
+    def c_near(s):
+        return send(0, s, piece(owner_of(s, corner), unit_of(s)), near.at[s], to_mate)
+
+    def c_mine(s):
+        return send(1, s, piece(mate, s), mine.at[s], to_mate)
+
+    def c_cross(s):
+        return send(2, s, outbox.at[s], inbox.at[s], to_across)
+
+    def c_twin(s):
+        r = pl.ds(s * UNIT, UNIT)
+        return send(3, s, ys.at[r], yr.at[r], to_twin)
+
+    def c_row(s):
+        return send(4, s, full.at[block(sq, s)], full.at[block(sq, s)], to_across)
+
+    def c_own(s):
+        r = block(owner_of(s, sq), unit_of(s))
+        return send(5, s, full.at[r], full.at[r], to_mate)
+
+    def c_pass(s):
+        return send(6, s, full.at[block(across, s)], full.at[block(across, s)], to_mate)
 
     def step_near(k):
-        c_near(k).start()
-        c_mine(k).start()
-
-    spot = lax.broadcasted_iota(jnp.int32, (heads, pos), 1)
+        for s in range(slots):
+            if unit_of(s) == k:
+                c_near(s).start()
+                if s < alone:
+                    c_mine(s).start()
 
     def step_values(k, pair, weights):
         for n, o in enumerate(pair):
@@ -268,12 +282,12 @@
                 dst[j] = jnp.dot(w, v2[(o * late + k - early) * UNIT + j], preferred_element_type=F32) + extra
 
     def step_attend(k, pair, before):
+        begin(halves.index((k, pair)) + AHEAD)
         for o in pair:
             for c in fetch(o, k):
                 c.wait()
         where = [(o, o * rows + k * UNIT + j, (o * late + k - early) * UNIT + j) for o in pair for j in range(UNIT)]
-        scores = [lax.dot_general(q_ref[b].astype(BF16), k2[n], (((1,), (1,)), ((), ())), preferred_element_type=F32)
-                  for _, b, n in where]
+        scores = [lax.dot_general(q_s[b].astype(BF16), k2[n], (((1,), (1,)), ((), ())), preferred_element_type=F32) for _, b, n in where]
         if before is not None:
             step_values(*before)
         weights = []
@@ -281,8 +295,8 @@
         for (o, b, _), sc in zip(where, scores):
             j = b % UNIT
             at = lens[b] - base
-            new = kv_ref[b:b + 1, :]
-            fresh = jnp.sum(q_ref[b] * new[:, :HEAD], axis=1, keepdims=True)
+            new = kv_s[b:b + 1, :]
+            fresh = jnp.sum(q_s[b] * new[:, :HEAD], axis=1, keepdims=True)
             here = spot == at
             sc = jnp.where(spot <= at, jnp.where(here, fresh, sc) * (HEAD ** -0.5), -1e30)
             top = jnp.max(sc, axis=1, keepdims=True)
@@ -296,62 +310,70 @@
             piece(o, k)[UNIT] = stats[o]
         return (k, pair, weights)
 
-    def step_merge(k):
-        c_near(k).wait_recv()
-        own = piece(across, k)
-        s0, s1 = own[UNIT], near[k, UNIT]
+    back = LANES - UNIT
+
+    def step_merge(s):
+        c_near(s).wait_recv()
+        own = piece(owner_of(s, across), unit_of(s))
+        s0, s1 = own[UNIT], near[s, UNIT]
         top = jnp.maximum(s0, s1)
         e0, e1 = jnp.exp(s0 - top), jnp.exp(s1 - top)
-        tot = pltpu.roll(s0, LANES - UNIT, 1) * e0 + pltpu.roll(s1, LANES - UNIT, 1) * e1
+        tot = pltpu.roll(s0, back, 1) * e0 + pltpu.roll(s1, back, 1) * e1
         for j in range(UNIT):
-            outbox[k, j] = own[j] * e0[:, j:j + 1] + near[k, j] * e1[:, j:j + 1]
-        outbox[k, UNIT] = jnp.where(lane < UNIT, top, jnp.where(lane < 2 * UNIT, pltpu.roll(tot, UNIT, 1), 0.0))
-        c_cross(k).start()
-
-    def step_combine(k):
-        c_mine(k).wait_recv()
-        c_cross(k).wait_recv()
-        own = piece(sq, k)
-        s0, s1, s2 = own[UNIT], mine[k, UNIT], inbox[k, UNIT]
-        top = jnp.maximum(jnp.maximum(s0, s1), s2)
-        e0, e1, e2 = jnp.exp(s0 - top), jnp.exp(s1 - top), jnp.exp(s2 - top)
-        back = LANES - UNIT
-        tot = pltpu.roll(s0, back, 1) * e0 + pltpu.roll(s1, back, 1) * e1 + pltpu.roll(s2, back, 1) * e2
+            outbox[s, j] = own[j] * e0[:, j:j + 1] + near[s, j] * e1[:, j:j + 1]
+        outbox[s, UNIT] = jnp.where(lane < UNIT, top, jnp.where(lane < 2 * UNIT, pltpu.roll(tot, UNIT, 1), 0.0))
+        c_cross(s).start()
+
+    def step_combine(s):
+        c_cross(s).wait_recv()
+        if s < alone:
+            c_mine(s).wait_recv()
+            boxes = [piece(sq, s), mine.at[s], inbox.at[s]]
+        else:
+            boxes = [outbox.at[s], inbox.at[s]]
+        stats = [b[UNIT] for b in boxes]
+        top = functools.reduce(jnp.maximum, stats)
+        scales = [jnp.exp(t - top) for t in stats]
+        tot = sum(pltpu.roll(t, back, 1) * e for t, e in zip(stats, scales))
         inv = 1.0 / jnp.where(lane < UNIT, tot, 1.0)
-        e0, e1, e2 = e0 * inv, e1 * inv, e2 * inv
+        scales = [e * inv for e in scales]
         for j in range(UNIT):
-            a_s[k * UNIT + j] = own[j] * e0[:, j:j + 1] + mine[k, j] * e1[:, j:j + 1] + inbox[k, j] * e2[:, j:j + 1]
-
-    def step_project(ks):
-        r = pl.ds(ks[0] * UNIT, len(ks) * UNIT)
+            a_s[s * UNIT + j] = sum(b[j] * e[:, j:j + 1] for b, e in zip(boxes, scales))
+
+    def step_project(ss_):
+        for s in ss_:
+            step_combine(s)
+        r = pl.ds(ss_[0] * UNIT, len(ss_) * UNIT)
         lhs = jnp.concatenate([a_s[r, h, :].astype(BF16) for h in range(heads)], axis=1)
-        ys[r, :] = jnp.dot(lhs, w_ref[...], preferred_element_type=F32)
-        for k in ks:
-            c_twin(k).start()
-
-    def step_rows(k):
-        c_twin(k).wait_recv()
-        r = pl.ds(k * UNIT, UNIT)
-        pair = x_ref[pl.ds(pl.multiple_of(sq * rows + (k // 2) * 2 * UNIT, 2 * UNIT), 2 * UNIT), :].astype(F32)
+        ys[r, :] = jnp.dot(lhs, wo_s[...], preferred_element_type=F32)
+        for s in ss_:
+            c_twin(s).start()
+
+    def step_rows(s):
+        c_twin(s).wait_recv()
+        r = pl.ds(s * UNIT, UNIT)
+        o, k = owner_of(s, sq), unit_of(s)
+        pair = x_s[pl.ds(pl.multiple_of(o * rows + (k // 2) * 2 * UNIT, 2 * UNIT), 2 * UNIT), :].astype(F32)
         half = pair[(k % 2) * UNIT:(k % 2 + 1) * UNIT]
-        full[block(sq, k), :] = half + (ys[r, :] + yr[r, :]) + b_ref[...]
-        c_row(k).start()
-        c_own(k).start()
-
-    def step_pass(k):
-        c_row(k).wait_recv()
-        c_pass(k).start()
-
-    def step_store(owner, k2):
-        r = pl.ds(pl.multiple_of(owner * rows + k2 * 2 * UNIT, 2 * UNIT), 2 * UNIT)
-        out[r, :] = full[r, :].astype(BF16)
+        full[block(o, k), :] = half + (ys[r, :] + yr[r, :]) + bo[...]
+        if s < alone:
+            c_row(s).start()
+        c_own(s).start()
+
+    def step_pass(s):
+        c_row(s).wait_recv()
+        c_pass(s).start()
+
+    def step_store(o):
+        for n in range(units // 2):
+            r = pl.ds(pl.multiple_of(o * rows + n * 2 * UNIT, 2 * UNIT), 2 * UNIT)
+            out[r, :] = full[r, :].astype(BF16)
 
     for k in range(early):
         step_near(k)
     get_lens.wait()
-    plan = PLAN[EARLY]
     before = None
-    for name, k in plan:
+    for name, k in PLAN:
         if name == "attend":
             k, half = k
             before = step_attend(k, ((0, 1), (2, 3))[half], before)
@@ -363,27 +385,22 @@
         elif name == "merge":
             step_merge(k)
         elif name == "project":
-            for n in k:
-                step_combine(n)
             step_project(k)
         elif name == "rows":
             step_rows(k)
         elif name == "pass":
             step_pass(k)
-        elif name == "store":
-            for n in range(units // 2):
-                step_store((sq, across)[k], n)
-    for n in range(units // 2):
-        for k in (2 * n, 2 * n + 1):
-            c_own(k).wait_recv()
-        step_store(mate, n)
-    for n in range(units // 2):
-        for k in (2 * n, 2 * n + 1):
-            c_pass(k).wait_recv()
-        step_store(corner, n)
-    for k in range(units):
-        for c in (c_near, c_mine, c_cross, c_twin, c_row, c_own, c_pass):
-            c(k).wait_send()
+    step_store(sq)
+    step_store(across)
+    for s in range(slots):
+        c_own(s).wait_recv()
+    step_store(mate)
+    for s in range(alone):
+        c_pass(s).wait_recv()
+    step_store(corner)
+    for s in range(slots):
+        for c in (c_near, c_cross, c_twin, c_own) + ((c_mine, c_row, c_pass) if s < alone else ()):
+            c(s).wait_send()
 
 
 def merge(part, q, kv, kc, vc, lens, w_out, hidden, b_out):
@@ -391,10 +408,11 @@
     seqs, width = hidden.shape
     rows = seqs // 4
     units = rows // UNIT
+    slots = units + SHARED
     left = seqs - 4 * EARLY * CHUNK
     vmem = pl.BlockSpec(memory_space=pltpu.VMEM)
     hbm = pl.BlockSpec(memory_space=pltpu.HBM)
-    box = pltpu.VMEM((units,) + part.shape[1:], F32)
+    box = pltpu.VMEM((slots,) + part.shape[1:], F32)
     pin = lambda a: pltpu.with_memory_space_constraint(a, pltpu.HBM)
     kept = pltpu.VMEM((left,) + kc.shape[1:], BF16)
     return pl.pallas_call(
@@ -404,8 +422,8 @@
         out_specs=(vmem, vmem, vmem),
         scratch_shapes=[
             pltpu.SMEM((seqs,), jnp.int32), pltpu.VMEM((left // UNIT,) + part.shape[1:], F32),
-            box, box, box, box, pltpu.VMEM((rows, heads, HEAD), F32), pltpu.VMEM((rows, width), F32), pltpu.VMEM((rows, width), F32),
-            pltpu.VMEM((4 * rows, width), F32), pltpu.SemaphoreType.DMA((7, units)), pltpu.SemaphoreType.DMA((7, units)),
+            box, box, box, box, pltpu.VMEM((slots * UNIT, heads, HEAD), F32), pltpu.VMEM((slots * UNIT, width), F32), pltpu.VMEM((slots * UNIT, width), F32),
+            pltpu.VMEM((4 * rows, width), F32), pltpu.SemaphoreType.DMA((7, slots)), pltpu.SemaphoreType.DMA((7, slots)),
             pltpu.SemaphoreType.DMA((left // UNIT,)), pltpu.SemaphoreType.DMA((left // UNIT,)), pltpu.SemaphoreType.DMA((1,)),
         ],
         compiler_params=pltpu.CompilerParams(collective_id=0, has_side_effects=True, vmem_limit_bytes=16 * 1024 * 1024),

time: 52.9 us -> 51.1 us (0.966)
  Pallas kernels: 52.1 us -> 50.1 us
    pallas_call x1, Pallas kernels: 20 us -> 14.3 us  [attend(): pl.pallas_call(functools.partial(attend_kernel, seqs), out_shape=(jax.Sha...]
    pallas_call x1, Pallas kernels: 4.18 us -> 6.77 us  [store(): pl.pallas_call(store_kernel, out_shape=(jax.ShapeDtypeStruct(kn.shape, BF...]
    pallas_call x1, Pallas kernels: 27.9 us -> 29 us  [merge(): pl.pallas_call(merge_kernel, out_shape=(jax.ShapeDtypeStruct(hidden.shape...]
where the time goes in v4:
time: 51.1 us; the launch traced here: 51 us
  Pallas kernels  50.1 us (98%)
  between operations  0.86 us (2%)
    pallas_call x1, Pallas kernels, merge(): pl.pallas_call(merge_kernel, out_shape=(jax.ShapeDtypeStruct(hidden.shape...  29 us
    pallas_call x1, Pallas kernels, attend(): pl.pallas_call(functools.partial(attend_kernel, seqs), out_shape=(jax.Sha...  14.3 us
    pallas_call x1, Pallas kernels, store(): pl.pallas_call(store_kernel, out_shape=(jax.ShapeDtypeStruct(kn.shape, BF...  6.77 us

profile of v4, /device:TPU:0, one launch (start us, length us, event | category | flops | bytes accessed | tf_op | source)
XLA Modules:
  0.0 51.0 jit_solution(16746297287077943998)
XLA Ops:
  0.6 0.0 copy-start
  0.6 0.0 copy-start.1
  0.7 0.0 copy-start.2
  0.7 14.3 %attend.1 = (bf16[256,256,128]{2,1,0:T(8,128)(2,1)}, bf16[256,256,128]{2,1,0:T(8,128)(2,1)}, f32[16,9,8,128]{3,2,1,0:T(8,128)S(1)}, f32[256,8,128]{2,1,0:T(8,128)S(1)}, f32[256,256]{1,0:T(8,128)S(1)}) custom-call(s32[256]{0:T(256)} %lens_hbm.5, bf16[256,2048]{1,0:T(8,128)(2,1)} %x_s.1, bf16[256,256,128]{2,1,0:T(8,128)(2,1)} %kc.3, ...), custom_call_target="tpu_custom_call" | custom-call | tf_op jit(solution)/shard_map/attend/pallas_call | solution.py:166
  15.0 0.0 copy-done
  15.0 0.0 copy-done.1
  15.0 0.0 copy-done.2
  15.0 29.0 %merge.1 = (bf16[256,2048]{1,0:T(8,128)(2,1)S(1)}, bf16[128,256,128]{2,1,0:T(8,128)(2,1)S(1)}, bf16[128,256,128]{2,1,0:T(8,128)(2,1)S(1)}) custom-call(f32[16,9,8,128]{3,2,1,0:T(8,128)S(1)} %get-tuple-element.15.part1, f32[256,8,128]{2,1,0:T(8,128)S(1)} %get-tuple-element.16.q_s, f32[256,256]{1,0:T(8,128)S(1)} %get-tuple-element.14.kv_s.kv, ...), custom_call_target="tpu_custom_call" | custom-call | tf_op jit(solution)/shard_map/merge/pallas_call | solution.py:418
  44.0 6.8 %store.1 = (bf16[256,256,128]{2,1,0:T(8,128)(2,1)}, bf16[256,256,128]{2,1,0:T(8,128)(2,1)}, bf16[256,2048]{1,0:T(8,128)(2,1)}, bf16[128,256,128]{2,1,0:T(8,128)(2,1)S(1)}, bf16[128,256,128]{2,1,0:T(8,128)(2,1)S(1)}) custom-call(f32[256,256]{1,0:T(8,128)S(1)} %get-tuple-element.14.kv_s.kv, ...), custom_call_target="tpu_custom_call", output_to_operand_aliasing={{3}: (3, {}), {4}: (4, {}), {0}: (5, {}), {1}: (6, {})} | custom-call | tf_op jit(solution)/shard_map/store/pallas_call | solution.py:474
Async XLA Ops:
  0.6 14.4 %copy-start = (bf16[1024,2048]{1,0:T(8,128)(2,1)S(1)}, bf16[1024,2048]{1,0:T(8,128)(2,1)}, u32[]{:S(2)}) copy-start(bf16[1024,2048]{1,0:T(8,128)(2,1)} %wo_s.1) | copy-start | bytes 12582916
  0.6 14.4 %copy-start.1 = (bf16[256,2048]{1,0:T(8,128)(2,1)S(1)}, bf16[256,2048]{1,0:T(8,128)(2,1)}, u32[]{:S(2)}) copy-start(bf16[256,2048]{1,0:T(8,128)(2,1)} %x_s.1) | copy-start | bytes 3145732
  0.7 14.4 %copy-start.2 = (f32[2048]{0:T(1024)S(1)}, f32[2048]{0:T(1024)}, u32[]{:S(2)}) copy-start(f32[2048]{0:T(1024)} %param.23) | copy-start | bytes 24580

commit v5 on v4

--- a/solution.py
+++ b/solution.py
@@ -10,21 +10,22 @@
 F32, BF16 = jnp.float32, jnp.bfloat16
 CHUNK = 16
 SLOTS = 14
-LEAD = 9
+LEAD = 12
 UNIT = 8
 GROUPS = CHUNK // UNIT
 AHEAD = 3
 EARLY = 2
 HEAD = 128
 LANES = 128
-SHARED = 1
+SOON = 2
+SHARED = 2
 PLAN = [
-    ("attend", (4, 0)), ("merge", 1), ("attend", (4, 1)), ("merge", 0), ("attend", (5, 0)), ("attend", (5, 1)), ("merge", 2),
-    ("merge", 3), ("merge", 4), ("attend", (6, 0)), ("project", [0, 1]), ("attend", (6, 1)), ("attend", (7, 0)),
-    ("merge", 5), ("attend", (7, 1)), ("merge", 6), ("values", 0), ("rows", 0), ("project", [2, 3]), ("rows", 1),
-    ("merge", 7), ("merge", 8), ("project", [4]), ("project", [5, 6]), ("rows", 2), ("rows", 3), ("project", [7]),
-    ("rows", 4), ("pass", 2), ("rows", 5), ("project", [8]), ("pass", 1), ("pass", 0), ("rows", 6), ("pass", 4), ("pass", 5),
-    ("pass", 3), ("rows", 8), ("rows", 7), ("pass", 6),
+    ("attend", (4, 0)), ("attend", (4, 1)), ("merge", 1), ("merge", 0), ("merge", 2), ("attend", (5, 0)), ("attend", (5, 1)),
+    ("attend", (6, 0)), ("merge", 3), ("attend", (6, 1)), ("project", [0, 1]), ("merge", 4), ("attend", (7, 0)),
+    ("merge", 5), ("project", [2, 3]), ("merge", 8), ("merge", 6), ("attend", (7, 1)), ("values", 0), ("rows", 0),
+    ("project", [4, 5]), ("merge", 9), ("rows", 1), ("merge", 7), ("project", [8]), ("rows", 2), ("project", [6]),
+    ("rows", 4), ("project", [9]), ("rows", 3), ("rows", 5), ("pass", 1), ("project", [7]), ("pass", 3), ("rows", 9),
+    ("rows", 6), ("rows", 8), ("pass", 2), ("pass", 4), ("pass", 0), ("pass", 5), ("rows", 7),
 ]
 
 
@@ -431,7 +432,7 @@
     )(part, q, kv, pin(kc), pin(vc), pin(lens), w_out, hidden, b_out[None])
 
 
-def store_kernel(kv, lens_hbm, y, k2_in, v2_in, kn_in, vn_in, kn, vn, y_out, k2, v2, lens, sem, wk, wv):
+def store_kernel(kv, lens_hbm, y, k2_in, v2_in, kn_in, vn_in, kn, vn, y_out, k2, v2, fix_k, fix_v, lens, sem, wk, wv, fk, fv):
     del k2_in, v2_in, kn_in, vn_in
     seqs, pos = kn.shape[:2]
     own = seqs // 4
@@ -442,27 +443,58 @@
     put_y = pltpu.make_async_copy(y, y_out, sem.at[1])
     get_lens.start()
     put_y.start()
+    places = [(o * own + own - left + n * CHUNK, o * left + n * CHUNK) for o in range(4) for n in range(left // CHUNK)]
+
+    def put(m):
+        first, kept = places[m]
+        src, dst = pl.ds(kept, CHUNK), pl.ds(first, CHUNK)
+        return pltpu.make_async_copy(k2.at[src], kn.at[dst], wk.at[m]), pltpu.make_async_copy(v2.at[src], vn.at[dst], wv.at[m])
+
+    def window(b):
+        slot = lens[b] - base
+        inside = jnp.logical_and(slot >= 0, slot < pos)
+        at = pl.multiple_of(jnp.where(inside, slot // 16, 0) * 16, 16)
+        return row16 == jnp.where(inside, slot - at, -1), pl.ds(at, 16)
+
+    def patch(m, j):
+        b = places[m][0] + j
+        _, win = window(b)
+        return (pltpu.make_async_copy(fix_k.at[m * CHUNK + j], kn.at[b, win], fk.at[m]),
+                pltpu.make_async_copy(fix_v.at[m * CHUNK + j], vn.at[b, win], fv.at[m]))
+
+    for m in range(SOON):
+        for c in put(m):
+            c.start()
     get_lens.wait()
-    pieces = []
-    for o in range(4):
-        for n in range(left // CHUNK):
-            first, kept = o * own + own - left + n * CHUNK, o * left + n * CHUNK
-            for j in range(CHUNK):
-                b = first + j
-                slot = lens[b] - base
-                inside = jnp.logical_and(slot >= 0, slot < pos)
-                at = pl.multiple_of(jnp.where(inside, slot // 16, 0) * 16, 16)
-                mark = row16 == jnp.where(inside, slot - at, -1)
-                win = pl.ds(at, 16)
-                new = kv[b:b + 1, :].astype(BF16)
-                k2[kept + j, win, :] = jnp.where(mark, new[:, :HEAD], k2[kept + j, win, :])
-                v2[kept + j, win, :] = jnp.where(mark, new[:, HEAD:], v2[kept + j, win, :])
-            src, dst, m = pl.ds(kept, CHUNK), pl.ds(first, CHUNK), len(pieces) // 2
-            pieces += [pltpu.make_async_copy(k2.at[src], kn.at[dst], wk.at[m]), pltpu.make_async_copy(v2.at[src], vn.at[dst], wv.at[m])]
-            pieces[-2].start()
-            pieces[-1].start()
-    for c in pieces:
-        c.wait()
+    for m in range(SOON, len(places)):
+        first, kept = places[m]
+        for j in range(CHUNK):
+            mark, win = window(first + j)
+            new = kv[first + j:first + j + 1, :].astype(BF16)
+            k2[kept + j, win, :] = jnp.where(mark, new[:, :HEAD], k2[kept + j, win, :])
+            v2[kept + j, win, :] = jnp.where(mark, new[:, HEAD:], v2[kept + j, win, :])
+        for c in put(m):
+            c.start()
+    for m in range(SOON):
+        first, kept = places[m]
+        for j in range(CHUNK):
+            mark, win = window(first + j)
+            new = kv[first + j:first + j + 1, :].astype(BF16)
+            fix_k[m * CHUNK + j] = jnp.where(mark, new[:, :HEAD], k2[kept + j, win, :])
+            fix_v[m * CHUNK + j] = jnp.where(mark, new[:, HEAD:], v2[kept + j, win, :])
+    for m in range(SOON):
+        for c in put(m):
+            c.wait()
+        for j in range(CHUNK):
+            for c in patch(m, j):
+                c.start()
+    for m in range(SOON, len(places)):
+        for c in put(m):
+            c.wait()
+    for m in range(SOON):
+        for j in range(CHUNK):
+            for c in patch(m, j):
+                c.wait()
     put_y.wait()
 
 
@@ -470,6 +502,7 @@
     vmem = pl.BlockSpec(memory_space=pltpu.VMEM)
     hbm = pl.BlockSpec(memory_space=pltpu.HBM)
     n = k2.shape[0] // CHUNK
+    fix = pltpu.VMEM((SOON * CHUNK, 16, HEAD), BF16)
     kept = pltpu.VMEM(k2.shape, BF16)
     return pl.pallas_call(
         store_kernel,
@@ -477,7 +510,8 @@
         in_specs=[vmem, hbm, vmem, vmem, vmem, hbm, hbm],
         out_specs=(hbm, hbm, hbm, vmem, vmem),
         input_output_aliases={3: 3, 4: 4, 5: 0, 6: 1},
-        scratch_shapes=[pltpu.SMEM(lens.shape, jnp.int32), pltpu.SemaphoreType.DMA((2,)), pltpu.SemaphoreType.DMA((n,)), pltpu.SemaphoreType.DMA((n,))],
+        scratch_shapes=[fix, fix, pltpu.SMEM(lens.shape, jnp.int32), pltpu.SemaphoreType.DMA((2,)), pltpu.SemaphoreType.DMA((n,)),
+                        pltpu.SemaphoreType.DMA((n,)), pltpu.SemaphoreType.DMA((SOON,)), pltpu.SemaphoreType.DMA((SOON,))],
         compiler_params=pltpu.CompilerParams(vmem_limit_bytes=4 * 1024 * 1024),
         name="store",
     )(kv, pltpu.with_memory_space_constraint(lens, pltpu.HBM), y, k2, v2, kn, vn)[:3]

time: 51.1 us -> 49.8 us (0.975)
  Pallas kernels: 50.1 us -> 48.8 us
    pallas_call x1, Pallas kernels: 29 us -> 27.9 us  [merge(): pl.pallas_call(merge_kernel, out_shape=(jax.ShapeDtypeStruct(hidden.shape...]
where the time goes in v5:
time: 49.8 us; the launch traced here: 49.7 us
  Pallas kernels  48.8 us (98%)
  between operations  0.86 us (2%)
    pallas_call x1, Pallas kernels, merge(): pl.pallas_call(merge_kernel, out_shape=(jax.ShapeDtypeStruct(hidden.shape...  27.9 us
    pallas_call x1, Pallas kernels, attend(): pl.pallas_call(functools.partial(attend_kernel, seqs), out_shape=(jax.Sha...  14.3 us
    pallas_call x1, Pallas kernels, store(): pl.pallas_call(store_kernel, out_shape=(jax.ShapeDtypeStruct(kn.shape, BF...  6.51 us

profile of v5, /device:TPU:0, one launch (start us, length us, event | category | flops | bytes accessed | tf_op | source)
XLA Modules:
  0.0 49.7 jit_solution(18288109761507585311)
XLA Ops:
  0.6 0.0 copy-start
  0.6 0.0 copy-start.1
  0.7 0.0 copy-start.2
  0.7 14.3 %attend.1 = (bf16[256,256,128]{2,1,0:T(8,128)(2,1)}, bf16[256,256,128]{2,1,0:T(8,128)(2,1)}, f32[16,9,8,128]{3,2,1,0:T(8,128)S(1)}, f32[256,8,128]{2,1,0:T(8,128)S(1)}, f32[256,256]{1,0:T(8,128)S(1)}) custom-call(s32[256]{0:T(256)} %lens_hbm.5, bf16[256,2048]{1,0:T(8,128)(2,1)} %x_s.1, bf16[256,256,128]{2,1,0:T(8,128)(2,1)} %kc.3, ...), custom_call_target="tpu_custom_call" | custom-call | tf_op jit(solution)/shard_map/attend/pallas_call | solution.py:167
  15.0 0.0 copy-done
  15.0 0.0 copy-done.1
  15.0 0.0 copy-done.2
  15.0 27.9 %merge.1 = (bf16[256,2048]{1,0:T(8,128)(2,1)S(1)}, bf16[128,256,128]{2,1,0:T(8,128)(2,1)S(1)}, bf16[128,256,128]{2,1,0:T(8,128)(2,1)S(1)}) custom-call(f32[16,9,8,128]{3,2,1,0:T(8,128)S(1)} %get-tuple-element.15.part1, f32[256,8,128]{2,1,0:T(8,128)S(1)} %get-tuple-element.16.q_s, f32[256,256]{1,0:T(8,128)S(1)} %get-tuple-element.14.kv_s.kv, ...), custom_call_target="tpu_custom_call" | custom-call | tf_op jit(solution)/shard_map/merge/pallas_call | solution.py:419
  43.0 6.5 %store.1 = (bf16[256,256,128]{2,1,0:T(8,128)(2,1)}, bf16[256,256,128]{2,1,0:T(8,128)(2,1)}, bf16[256,2048]{1,0:T(8,128)(2,1)}, bf16[128,256,128]{2,1,0:T(8,128)(2,1)S(1)}, bf16[128,256,128]{2,1,0:T(8,128)(2,1)S(1)}) custom-call(f32[256,256]{1,0:T(8,128)S(1)} %get-tuple-element.14.kv_s.kv, ...), custom_call_target="tpu_custom_call", output_to_operand_aliasing={{3}: (3, {}), {4}: (4, {}), {0}: (5, {}), {1}: (6, {})} | custom-call | tf_op jit(solution)/shard_map/store/pallas_call | solution.py:507
Async XLA Ops:
  0.6 14.4 %copy-start = (bf16[1024,2048]{1,0:T(8,128)(2,1)S(1)}, bf16[1024,2048]{1,0:T(8,128)(2,1)}, u32[]{:S(2)}) copy-start(bf16[1024,2048]{1,0:T(8,128)(2,1)} %wo_s.1) | copy-start | bytes 12582916
  0.6 14.4 %copy-start.1 = (bf16[256,2048]{1,0:T(8,128)(2,1)S(1)}, bf16[256,2048]{1,0:T(8,128)(2,1)}, u32[]{:S(2)}) copy-start(bf16[256,2048]{1,0:T(8,128)(2,1)} %x_s.1) | copy-start | bytes 3145732
  0.7 14.4 %copy-start.2 = (f32[2048]{0:T(1024)S(1)}, f32[2048]{0:T(1024)}, u32[]{:S(2)}) copy-start(f32[2048]{0:T(1024)} %param.23) | copy-start | bytes 24580

commit v6 on v5

--- a/solution.py
+++ b/solution.py
@@ -13,7 +13,7 @@
 LEAD = 12
 UNIT = 8
 GROUPS = CHUNK // UNIT
-AHEAD = 3
+AHEAD = 2
 EARLY = 2
 HEAD = 128
 LANES = 128

time: 49.8 us -> 49.9 us (level)
  no operation moved by 1% of the time
where the time goes in v6:
time: 49.9 us; the launch traced here: 49.8 us
  Pallas kernels  48.9 us (98%)
  between operations  0.86 us (2%)
    pallas_call x1, Pallas kernels, merge(): pl.pallas_call(merge_kernel, out_shape=(jax.ShapeDtypeStruct(hidden.shape...  28.1 us
    pallas_call x1, Pallas kernels, attend(): pl.pallas_call(functools.partial(attend_kernel, seqs), out_shape=(jax.Sha...  14.3 us
    pallas_call x1, Pallas kernels, store(): pl.pallas_call(store_kernel, out_shape=(jax.ShapeDtypeStruct(kn.shape, BF...  6.51 us

profile of v6, /device:TPU:0, one launch (start us, length us, event | category | flops | bytes accessed | tf_op | source)
XLA Modules:
  0.0 49.8 jit_solution(9543248081152789650)
XLA Ops:
  0.6 0.0 copy-start
  0.6 0.0 copy-start.1
  0.7 0.0 copy-start.2
  0.7 14.3 %attend.1 = (bf16[256,256,128]{2,1,0:T(8,128)(2,1)}, bf16[256,256,128]{2,1,0:T(8,128)(2,1)}, f32[16,9,8,128]{3,2,1,0:T(8,128)S(1)}, f32[256,8,128]{2,1,0:T(8,128)S(1)}, f32[256,256]{1,0:T(8,128)S(1)}) custom-call(s32[256]{0:T(256)} %lens_hbm.5, bf16[256,2048]{1,0:T(8,128)(2,1)} %x_s.1, bf16[256,256,128]{2,1,0:T(8,128)(2,1)} %kc.3, ...), custom_call_target="tpu_custom_call" | custom-call | tf_op jit(solution)/shard_map/attend/pallas_call | solution.py:167
  15.0 0.0 copy-done
  15.0 0.0 copy-done.1
  15.0 0.0 copy-done.2
  15.0 28.1 %merge.1 = (bf16[256,2048]{1,0:T(8,128)(2,1)S(1)}, bf16[128,256,128]{2,1,0:T(8,128)(2,1)S(1)}, bf16[128,256,128]{2,1,0:T(8,128)(2,1)S(1)}) custom-call(f32[16,9,8,128]{3,2,1,0:T(8,128)S(1)} %get-tuple-element.15.part1, f32[256,8,128]{2,1,0:T(8,128)S(1)} %get-tuple-element.16.q_s, f32[256,256]{1,0:T(8,128)S(1)} %get-tuple-element.14.kv_s.kv, ...), custom_call_target="tpu_custom_call" | custom-call | tf_op jit(solution)/shard_map/merge/pallas_call | solution.py:419
  43.1 6.5 %store.1 = (bf16[256,256,128]{2,1,0:T(8,128)(2,1)}, bf16[256,256,128]{2,1,0:T(8,128)(2,1)}, bf16[256,2048]{1,0:T(8,128)(2,1)}, bf16[128,256,128]{2,1,0:T(8,128)(2,1)S(1)}, bf16[128,256,128]{2,1,0:T(8,128)(2,1)S(1)}) custom-call(f32[256,256]{1,0:T(8,128)S(1)} %get-tuple-element.14.kv_s.kv, ...), custom_call_target="tpu_custom_call", output_to_operand_aliasing={{3}: (3, {}), {4}: (4, {}), {0}: (5, {}), {1}: (6, {})} | custom-call | tf_op jit(solution)/shard_map/store/pallas_call | solution.py:507
Async XLA Ops:
  0.6 14.4 %copy-start = (bf16[1024,2048]{1,0:T(8,128)(2,1)S(1)}, bf16[1024,2048]{1,0:T(8,128)(2,1)}, u32[]{:S(2)}) copy-start(bf16[1024,2048]{1,0:T(8,128)(2,1)} %wo_s.1) | copy-start | bytes 12582916
  0.6 14.4 %copy-start.1 = (bf16[256,2048]{1,0:T(8,128)(2,1)S(1)}, bf16[256,2048]{1,0:T(8,128)(2,1)}, u32[]{:S(2)}) copy-start(bf16[256,2048]{1,0:T(8,128)(2,1)} %x_s.1) | copy-start | bytes 3145732
  0.7 14.4 %copy-start.2 = (f32[2048]{0:T(1024)S(1)}, f32[2048]{0:T(1024)}, u32[]{:S(2)}) copy-start(f32[2048]{0:T(1024)} %param.23) | copy-start | bytes 24580
